TPU v7x, 32 devices: a whole 2x2x4 slice. The times are simulated.
32 devices in a mesh: tile: 8 (over y, x, core), head: 4 (over z).
Axes of the slice: x: 2, y: 2, z: 4, core: 2. Of those that a mesh axis runs over, the one named last changes fastest.
Arguments:
- latent: bfloat16 [16, 512, 512], P('tile', 'head'), may hold values from -6 to 6
- norm1_gain: float32 [512], replicated, may hold values from 0.25 to 1.75
- norm1_shift: float32 [512], replicated, may hold values from -1.75 to 1.75
- conv1_weight: bfloat16 [3, 3, 512, 512], replicated, may hold values from -0.09375 to 0.09375
- conv1_bias: float32 [512], replicated, may hold values from -1.75 to 1.75
- norm2_gain: float32 [512], replicated, may hold values from 0.25 to 1.75
- norm2_shift: float32 [512], replicated, may hold values from -1.75 to 1.75
- conv2_weight: bfloat16 [3, 3, 512, 512], replicated, may hold values from -0.09375 to 0.09375
- conv2_bias: float32 [512], replicated, may hold values from -1.75 to 1.75
- norm3_gain: float32 [512], replicated, may hold values from 0.25 to 1.75
- norm3_shift: float32 [512], replicated, may hold values from -1.75 to 1.75
- query_weight: bfloat16 [512, 512], replicated, may hold values from -2 to 2
- query_bias: float32 [512], replicated, may hold values from -3 to 3
- key_weight: bfloat16 [512, 512], replicated, may hold values from -2 to 2
- value_weight: bfloat16 [512, 512], replicated, may hold values from -0.25 to 0.25
- value_bias: float32 [512], replicated, may hold values from -3 to 3
- out_weight: bfloat16 [512, 512], replicated, may hold values from -0.5 to 0.5
- out_bias: float32 [512], replicated, may hold values from -1.75 to 1.75
Outputs:
- block_out: bfloat16 [16, 512, 512], P('tile', 'head')
All inputs are finite; a program needn't handle non-finite values.
Results may differ from a plain program's by a relative error of at most 0.01615.
Values may be sent and summed in bfloat16 or wider, within the bound.
A program may use at most 128 MiB of HBM per device.

v0:
```python
import jax
import jax.numpy as jnp
from jax import lax
from jax.sharding import PartitionSpec as P

C = 512
GROUPS = 32


def extended(x, sides, width):
    for axis, dim in sides:
        peers, length = (lax.axis_size(axis), x.shape[dim])
        up = [(i, (i + 1) % peers) for i in range(peers - 1)]
        down = [(j, i) for i, j in up]
        last = lax.slice_in_dim(x, length - width, length, axis=dim)
        initial = lax.slice_in_dim(x, 0, width, axis=dim)
        before = lax.ppermute(last, axis, up)
        after = lax.ppermute(initial, axis, down)
        x = jnp.concatenate([before, x, after], axis=dim)
    return x


def group_norm(values, gain, shift, members):
    grouped = values.reshape(-1, GROUPS, C // GROUPS)
    sums = lax.psum(jnp.sum(grouped, axis=(0, 2)), ("tile", "head"))
    mean = sums / members
    deviation = grouped - mean[None, :, None]
    variance = lax.psum(jnp.sum(deviation * deviation, axis=(0, 2)), ("tile", "head")) / members
    normalized = deviation * lax.rsqrt(variance + 1e-06)[None, :, None]
    return normalized.reshape(values.shape) * gain + shift


def conv_three(act, weight, bias):
    padded = extended(act, (("tile", 0), ("head", 1)), 1)
    result = lax.conv_general_dilated(
        padded[None],
        weight,
        (1, 1),
        "VALID",
        dimension_numbers=("NHWC", "HWIO", "NHWC"),
        preferred_element_type=jnp.float32,
    )[0]
    return result + bias


def per_device(
    latent,
    norm1_gain,
    norm1_shift,
    conv1_weight,
    conv1_bias,
    norm2_gain,
    norm2_shift,
    conv2_weight,
    conv2_bias,
    norm3_gain,
    norm3_shift,
    query_weight,
    query_bias,
    key_weight,
    value_weight,
    value_bias,
    out_weight,
    out_bias,
):
    local_rows, local_cols, channels = latent.shape
    positions = local_rows * local_cols
    members = positions * lax.axis_size("tile") * lax.axis_size("head") * (C // GROUPS)
    latent32 = latent.astype(jnp.float32).reshape(positions, C)
    act1 = jax.nn.silu(group_norm(latent32, norm1_gain, norm1_shift, members)).astype(jnp.bfloat16)
    hidden = conv_three(act1.reshape(local_rows, local_cols, C), conv1_weight, conv1_bias).reshape(
        positions, C
    )
    act2 = jax.nn.silu(group_norm(hidden, norm2_gain, norm2_shift, members)).astype(jnp.bfloat16)
    second = conv_three(act2.reshape(local_rows, local_cols, C), conv2_weight, conv2_bias).reshape(
        positions, C
    )
    resid = (latent32 + second).astype(jnp.bfloat16)
    normed = group_norm(resid.astype(jnp.float32), norm3_gain, norm3_shift, members).astype(
        jnp.bfloat16
    )
    queries = (
        jnp.dot(normed, query_weight, preferred_element_type=jnp.float32) + query_bias
    ).astype(jnp.bfloat16)
    tile_queries = lax.all_gather(queries, "head", axis=0, tiled=True)
    query_rows = tile_queries.shape[0]
    softmax_scale = 1.0 / C**0.5
    widest = positions * max(1, 2048 // positions)
    initial = (
        jnp.full((query_rows,), -1e30, jnp.float32),
        jnp.zeros((query_rows,), jnp.float32),
        jnp.zeros((query_rows, C), jnp.float32),
    )
    keys = jnp.dot(normed, key_weight, preferred_element_type=jnp.float32).astype(jnp.bfloat16)
    values = (
        jnp.dot(normed, value_weight, preferred_element_type=jnp.float32) + value_bias
    ).astype(jnp.bfloat16)
    key_rows = lax.all_gather(keys, "tile", axis=0, tiled=True)
    rows_here = key_rows.shape[0]
    block_len = min(rows_here, widest)
    while rows_here % block_len != 0:
        block_len = block_len - positions
    nblocks = rows_here // block_len

    def step_block(state_in, block_pair):
        run_max, run_sum, weighted = state_in
        key_block, value_block = block_pair
        scores = (
            jnp.dot(tile_queries, key_block.T, preferred_element_type=jnp.float32) * softmax_scale
        )
        new_max = jnp.maximum(run_max, jnp.max(scores, axis=1))
        factor = jnp.exp(run_max - new_max)
        expo = jnp.exp(scores - new_max[:, None])
        run_sum = run_sum * factor + jnp.sum(expo, axis=1)
        weighted = weighted * factor[:, None] + jnp.dot(
            expo.astype(jnp.bfloat16), value_block, preferred_element_type=jnp.float32
        )
        return ((new_max, run_sum, weighted), None)

    blocked = (
        key_rows.reshape(nblocks, block_len, C),
        lax.all_gather(values, "tile", axis=0, tiled=True).reshape(nblocks, block_len, C),
    )
    state_out, unused = lax.scan(step_block, initial, blocked)
    run_max, run_sum, weighted = state_out
    top = lax.pmax(run_max, "head")
    factor = jnp.exp(run_max - top)
    own_weighted, own_sum = (
        lax.psum_scatter(
            (weighted * factor[:, None]).astype(jnp.bfloat16),
            "head",
            scatter_dimension=0,
            tiled=True,
        ).astype(jnp.float32),
        lax.psum_scatter(
            (run_sum * factor).astype(jnp.bfloat16), "head", scatter_dimension=0, tiled=True
        ).astype(jnp.float32),
    )
    attended = (own_weighted / own_sum[:, None]).astype(jnp.bfloat16)
    mixed = (
        resid.astype(jnp.float32)
        + jnp.dot(attended, out_weight, preferred_element_type=jnp.float32)
        + out_bias
    )
    return mixed.astype(jnp.bfloat16).reshape(local_rows, local_cols, C)


def solution(mesh):
    return jax.shard_map(
        per_device,
        mesh=mesh,
        in_specs=(
            P("tile", "head", None),
            P(),
            P(),
            P(),
            P(),
            P(),
            P(),
            P(),
            P(),
            P(),
            P(),
            P(),
            P(),
            P(),
            P(),
            P(),
            P(),
            P(),
        ),
        out_specs=P("tile", "head", None),
        check_vma=False,
    )
```

profile of v0, /device:TPU:8, one launch (start us, length us, event | category | flops | bytes accessed | tf_op | source)
XLA Modules:
  0.0 425.7 jit_solution(8962881131567020059)
XLA Ops:
  6.5 1.1 convert_reduce_fusion.1
  7.8 40.5 %psum.42 = f32[32]{0:T(128)S(1)} all-reduce(f32[32]{0:T(128)S(1)} %reduce_sum.83), channel_id=1, replica_groups=mesh['tile'=8,'head'=4] {'tile','head'}, use_global_device_ids=true, to_apply=%region_2.0 | all-reduce | flops 32 | bytes 256 | tf_op jit(solution)/shard_map/psum | solution.py:25
  48.4 1.0 fusion.46
  49.7 39.1 %psum.43 = f32[32]{0:T(128)S(1)} all-reduce(f32[32]{0:T(128)S(1)} %reduce_sum.89), channel_id=1, replica_groups=mesh['tile'=8,'head'=4] {'tile','head'}, use_global_device_ids=true, to_apply=%region_5.6 | all-reduce | flops 32 | bytes 256 | tf_op jit(solution)/shard_map/psum | solution.py:28
  88.9 1.2 fusion.63
  90.1 1.3 collective-permute-start
  91.4 1.3 collective-permute-start.1
  92.7 1.2 fusion.54
  93.9 3.3 collective-permute-done.1
  97.2 3.4 collective-permute-start.2
  100.6 2.7 collective-permute-start.3
  103.3 2.8 collective-permute-done.3
  106.3 0.3 copy.59
  106.6 0.2 pad.clone
  107.0 1.5 select_reduce_fusion.1
  108.7 41.3 %psum.44 = f32[32]{0:T(128)S(1)} all-reduce(f32[32]{0:T(128)S(1)} %reduce_sum.92), channel_id=1, replica_groups=mesh['tile'=8,'head'=4] {'tile','head'}, use_global_device_ids=true, to_apply=%region_8.9 | all-reduce | flops 32 | bytes 256 | tf_op jit(solution)/shard_map/psum | solution.py:25
  150.1 0.2 select_reduce_fusion
  150.5 0.4 copy.50
  150.9 40.9 %psum.45 = f32[32]{0:T(128)S(1)} all-reduce(f32[32]{0:T(128)S(1)} %reduce_sum.117), channel_id=1, replica_groups=mesh['tile'=8,'head'=4] {'tile','head'}, use_global_device_ids=true, to_apply=%region_11.12 | all-reduce | flops 32 | bytes 256 | tf_op jit(solution)/shard_map/psum | solution.py:28
  192.2 0.2 multiply_convert_fusion.2
  192.4 1.3 collective-permute-start.4
  193.7 1.3 collective-permute-start.5
  195.0 0.2 multiply_convert_fusion.1
  195.2 4.2 collective-permute-done.5
  199.5 3.3 collective-permute-start.6
  202.8 2.5 collective-permute-start.7
  205.3 3.0 collective-permute-done.7
  208.5 0.3 copy.60
  208.8 0.2 pad.2.clone
  209.1 3.8 convolution_select_fusion
  213.0 0.4 copy.55
  213.5 0.4 copy-done.1
  214.2 40.8 %psum.46 = f32[32]{0:T(128)S(1)} all-reduce(f32[32]{0:T(128)S(1)} %reduce_sum.120), channel_id=1, replica_groups=mesh['tile'=8,'head'=4] {'tile','head'}, use_global_device_ids=true, to_apply=%region_14.15 | all-reduce | flops 32 | bytes 256 | tf_op jit(solution)/shard_map/psum | solution.py:25
  255.6 41.3 %psum.47 = f32[32]{0:T(128)S(1)} all-reduce(f32[32]{0:T(128)S(1)} %reduce_sum.123), channel_id=1, replica_groups=mesh['tile'=8,'head'=4] {'tile','head'}, use_global_device_ids=true, to_apply=%region_17.18 | all-reduce | flops 32 | bytes 256 | tf_op jit(solution)/shard_map/psum | solution.py:28
  297.1 1.0 fusion.12
  298.2 1.0 convolution_convert_fusion
  299.3 1.0 fusion.13
  300.4 24.9 %all-gather.4.cloned.1.call-done = bf16[1024,512]{1,0:T(8,128)(2,1)} async-done(((bf16[256,512]{1,0:T(8,128)(2,1)}), bf16[1024,512]{1,0:T(8,128)(2,1)}) %all-gather.4.cloned.1.call-update) | async-done | bytes 1048592 | tf_op jit(solution)/shard_map/all_gather | solution.py:85
  325.4 29.1 %all-gather.6.cloned.1.call-done = bf16[2048,512]{1,0:T(8,128)(2,1)} async-done(((bf16[256,512]{1,0:T(8,128)(2,1)}), bf16[2048,512]{1,0:T(8,128)(2,1)}) %all-gather.6.cloned.1.call-update) | async-done | bytes 2097168 | tf_op jit(solution)/shard_map/all_gather | solution.py:98
  354.5 7.5 %multiply_reduce_fusion = (f32[1024]{0:T(1024)S(1)}, f32[1024,2048]{1,0:T(8,128)}) fusion(bf16[1024,512]{1,0:T(8,128)(2,1)} %all-gather.4.cloned.1.call-done, bf16[2048,512]{1,0:T(8,128)(2,1)} %all-gather.6.cloned.1.call-done), kind=kOutput, calls=%fused_computation.1 | convolution fusion | flops 2151676928 | bytes 11538432 | tf_op jit(solution)/shard_map/while/body/eval_jaxpr/dot_general | solution.py:109
  362.0 8.9 %pmax.7 = f32[1024]{0:T(1024)S(1)} all-reduce(f32[1024]{0:T(1024)S(1)} %broadcast_maximum_fusion), channel_id=1, replica_groups=mesh['tile'=8,'head'=4] {'head'}, use_global_device_ids=true, to_apply=%region_19.20 | all-reduce | flops 1024 | bytes 8192 | tf_op jit(solution)/shard_map/pmax | solution.py:126
  370.9 4.4 %fusion = f32[1024]{0:T(1024)S(1)} fusion(f32[1024,2048]{1,0:T(8,128)} %get-tuple-element.42, f32[1024]{0:T(1024)S(1)} %broadcast_maximum_fusion), kind=kLoop, calls=%fused_computation.2 | loop fusion | flops 6290432 | bytes 8396800 | tf_op jit(solution)/shard_map/while/body/eval_jaxpr/reduce_sum | solution.py:114
  375.3 8.9 %all-gather.8.cloned.1.call-done = bf16[2048,512]{1,0:T(8,128)(2,1)} async-done(((bf16[256,512]{1,0:T(8,128)(2,1)}), bf16[2048,512]{1,0:T(8,128)(2,1)}) %all-gather.8.cloned.1.call-update) | async-done | bytes 2097168 | tf_op jit(solution)/shard_map/all_gather | solution.py:122
  384.2 7.4 %multiply_convert_fusion = bf16[1024,512]{1,0:T(8,128)(2,1)} fusion(bf16[2048,512]{1,0:T(8,128)(2,1)} %all-gather.8.cloned.1.call-done, f32[1024,2048]{1,0:T(8,128)} %get-tuple-element.42, f32[1024]{0:T(1024)S(1)} %broadcast_maximum_fusion, f32[1024]{0:T(1024)S(1)} %get-tuple-element.18, f32[1024]{0:T(1024)S(1)} %get-tuple-element.38), kind=kOutput, calls=%fused_computation.7 | convolution fusion | flops 2155347968 | bytes 11546624 | tf_op jit(solution)/shard_map/while/body/eval_jaxpr/dot_general | solution.py:115
  391.6 0.6 dynamic-slice.2
  392.9 9.1 %all-reduce = bf16[1024]{0:T(1024)(128)(2,1)S(1)} all-reduce(bf16[1024]{0:T(1024)(128)(2,1)S(1)} %get-tuple-element.17), channel_id=3, replica_groups=mesh['tile'=8,'head'=4] {'head'}, use_global_device_ids=true, to_apply=%region_22.23.clone | all-reduce | flops 1024 | bytes 4096
  402.1 15.0 %reduce-scatter.2.cloned.1.call-done = bf16[256,512]{1,0:T(8,128)(2,1)} async-done(((bf16[1024,512]{1,0:T(8,128)(2,1)}), bf16[256,512]{1,0:T(8,128)(2,1)}) %reduce-scatter.2.cloned.1.call-update) | async-done | bytes 262160 | tf_op jit(solution)/shard_map/reduce_scatter | solution.py:129
  417.1 2.0 fusion.11
  (95 shorter events, 3.7 us)
Async XLA Ops:
  6.5 290.6 %copy-start = (bf16[512,512]{1,0:T(8,128)(2,1)S(1)}, bf16[512,512]{1,0:T(8,128)(2,1)}, u32[]{:S(2)}) copy-start(bf16[512,512]{1,0:T(8,128)(2,1)} %param.29) | copy-start | bytes 1572868
  6.5 318.8 %all-gather.4.cloned.1.call-start = ((), (), s32[]{:S(2)}) async-start(), calls=%async_computation.1 | async-start | bytes 1310720 | tf_op jit(solution)/shard_map/all_gather | solution.py:85
  90.1 3.8 collective-permute-start
  91.4 5.7 %collective-permute-start.1 = (bf16[1,128,512]{2,1,0:T(8,128)(2,1)S(1)}, bf16[1,128,512]{2,1,0:T(8,128)(2,1)S(1)}, u32[]{:S(2)}, u32[]{:S(2)}) collective-permute-start(bf16[1,128,512]{2,1,0:T(8,128)(2,1)S(1)} %get-tuple-element.37), channel_id=1, source_target_pairs={{4,0},{8,4},{12,8},{16,12},{20,16},{24,20},{28,24},{5,1},{9,5},{13... | collective-permute-start | bytes 393224 | tf_op jit(solution)/shard_map/ppermute | solution.py:18
  97.2 9.8 %copy-start.7 = (bf16[3,3,512,512]{3,2,1,0:T(8,128)(2,1)S(1)}, bf16[3,3,512,512]{3,2,1,0:T(8,128)(2,1)}, u32[]{:S(2)}) copy-start(bf16[3,3,512,512]{3,2,1,0:T(8,128)(2,1)} %param.21) | copy-start | bytes 14155780
  97.2 6.1 %collective-permute-start.2 = (bf16[4,1,512]{2,1,0:T(2,128)(2,1)S(1)}, bf16[4,1,512]{2,1,0:T(2,128)(2,1)S(1)}, u32[]{:S(2)}, u32[]{:S(2)}) collective-permute-start(bf16[4,1,512]{2,1,0:T(2,128)(2,1)S(1)} %get-tuple-element.32), channel_id=1, source_target_pairs={{0,1},{1,2},{2,3},{4,5},{5,6},{6,7},{8,9},{9,10},{10,11},{12,13},{... | collective-permute-start | bytes 12296 | tf_op jit(solution)/shard_map/ppermute | solution.py:17
  100.6 6.4 %copy-start.2 = (f32[512]{0:T(512)S(1)}, f32[512]{0:T(512)}, u32[]{:S(2)}) copy-start(f32[512]{0:T(512)} %param.22) | copy-start | bytes 6148
  100.6 6.4 %copy-start.6 = (pred[8,17]{0,1:T(8,128)(4,1)S(1)}, pred[8,17]{0,1:T(8,128)(4,1)}, u32[]{:S(2)}) copy-start(pred[8,17]{0,1:T(8,128)(4,1)} %constant.47) | copy-start | bytes 412
  100.6 5.5 %collective-permute-start.3 = (bf16[4,1,512]{2,1,0:T(2,128)(2,1)S(1)}, bf16[4,1,512]{2,1,0:T(2,128)(2,1)S(1)}, u32[]{:S(2)}, u32[]{:S(2)}) collective-permute-start(bf16[4,1,512]{2,1,0:T(2,128)(2,1)S(1)} %get-tuple-element.33), channel_id=1, source_target_pairs={{1,0},{2,1},{3,2},{5,4},{6,5},{7,6},{9,8},{10,9},{11,10},{13,12},{... | collective-permute-start | bytes 12296 | tf_op jit(solution)/shard_map/ppermute | solution.py:18
  108.5 83.7 %copy-start.3 = (f32[512]{0:T(512)S(1)}, f32[512]{0:T(512)}, u32[]{:S(2)}) copy-start(f32[512]{0:T(512)} %param.24) | copy-start | bytes 6148
  108.5 83.7 %copy-start.4 = (f32[512]{0:T(512)S(1)}, f32[512]{0:T(512)}, u32[]{:S(2)}) copy-start(f32[512]{0:T(512)} %param.23) | copy-start | bytes 6148
  192.4 2.8 collective-permute-start.4
  193.7 5.7 %collective-permute-start.5 = (bf16[1,128,512]{2,1,0:T(8,128)(2,1)S(1)}, bf16[1,128,512]{2,1,0:T(8,128)(2,1)S(1)}, u32[]{:S(2)}, u32[]{:S(2)}) collective-permute-start(bf16[1,128,512]{2,1,0:T(8,128)(2,1)S(1)} %get-tuple-element.35), channel_id=1, source_target_pairs={{4,0},{8,4},{12,8},{16,12},{20,16},{24,20},{28,24},{5,1},{9,5},{13... | collective-permute-start | bytes 393224 | tf_op jit(solution)/shard_map/ppermute | solution.py:18
  199.5 5.9 %collective-permute-start.6 = (bf16[4,1,512]{2,1,0:T(2,128)(2,1)S(1)}, bf16[4,1,512]{2,1,0:T(2,128)(2,1)S(1)}, u32[]{:S(2)}, u32[]{:S(2)}) collective-permute-start(bf16[4,1,512]{2,1,0:T(2,128)(2,1)S(1)} %get-tuple-element.28), channel_id=1, source_target_pairs={{0,1},{1,2},{2,3},{4,5},{5,6},{6,7},{8,9},{9,10},{10,11},{12,13},{... | collective-permute-start | bytes 12296 | tf_op jit(solution)/shard_map/ppermute | solution.py:17
  202.8 5.5 %collective-permute-start.7 = (bf16[4,1,512]{2,1,0:T(2,128)(2,1)S(1)}, bf16[4,1,512]{2,1,0:T(2,128)(2,1)S(1)}, u32[]{:S(2)}, u32[]{:S(2)}) collective-permute-start(bf16[4,1,512]{2,1,0:T(2,128)(2,1)S(1)} %get-tuple-element.30), channel_id=1, source_target_pairs={{1,0},{2,1},{3,2},{5,4},{6,5},{7,6},{9,8},{10,9},{11,10},{13,12},{... | collective-permute-start | bytes 12296 | tf_op jit(solution)/shard_map/ppermute | solution.py:18
  212.9 1.0 copy-start.1
  212.9 0.9 copy-start.5
  213.4 83.7 %copy-start.11 = (f32[512]{0:T(512)S(1)}, f32[512]{0:T(512)}, u32[]{:S(2)}) copy-start(f32[512]{0:T(512)} %param.30) | copy-start | bytes 6148
  213.4 83.7 %copy-start.12 = (f32[512]{0:T(512)S(1)}, f32[512]{0:T(512)}, u32[]{:S(2)}) copy-start(f32[512]{0:T(512)} %param.28) | copy-start | bytes 6148
  213.4 83.7 %copy-start.13 = (f32[512]{0:T(512)S(1)}, f32[512]{0:T(512)}, u32[]{:S(2)}) copy-start(f32[512]{0:T(512)} %param.27) | copy-start | bytes 6148
  255.1 43.1 %copy-start.8 = (bf16[512,512]{1,0:T(8,128)(2,1)S(1)}, bf16[512,512]{1,0:T(8,128)(2,1)}, u32[]{:S(2)}) copy-start(bf16[512,512]{1,0:T(8,128)(2,1)} %param.31) | copy-start | bytes 1572868
  297.0 2.3 copy-start.9
  297.0 2.3 copy-start.14
  298.2 56.3 %all-gather.6.cloned.1.call-start = ((), (), s32[]{:S(2)}) async-start(), calls=%async_computation.2 | async-start | bytes 2359296 | tf_op jit(solution)/shard_map/all_gather | solution.py:98
  299.3 84.9 %all-gather.8.cloned.1.call-start = ((), (), s32[]{:S(2)}) async-start(), calls=%async_computation.3 | async-start | bytes 2359296 | tf_op jit(solution)/shard_map/all_gather | solution.py:122
  300.4 116.7 %reduce-scatter.2.cloned.1.call-start = ((), (), s32[]{:S(2)}) async-start(), calls=%async_computation.4 | async-start | bytes 1310720 | tf_op jit(solution)/shard_map/reduce_scatter | solution.py:129
  384.2 7.4 %copy-start.16 = (u32[32]{0:T(128)S(1)}, u32[32]{0:T(128)}, u32[]{:S(2)}) copy-start(u32[32]{0:T(128)} %constant.53) | copy-start | bytes 388
  384.2 32.9 %copy-start.10 = (bf16[512,512]{1,0:T(8,128)(2,1)S(1)}, bf16[512,512]{1,0:T(8,128)(2,1)}, u32[]{:S(2)}) copy-start(bf16[512,512]{1,0:T(8,128)(2,1)} %param.34) | copy-start | bytes 1572868
  384.2 32.9 %copy-start.15 = (f32[512]{0:T(512)S(1)}, f32[512]{0:T(512)}, u32[]{:S(2)}) copy-start(f32[512]{0:T(512)} %param.35) | copy-start | bytes 6148
Sparse Core Ops, SparseCore 0:
  298.3 27.0 all-gather.3
  327.3 27.1 all-gather.5
  356.4 27.7 all-gather.7
  391.8 25.3 reduce-scatter.1
where the time goes:
time: 430 us; the launch traced here: 426 us
  blocking collectives  262 us (61%)
  waiting for transfers between devices  91.3 us (21%)
  matrix products  25.3 us (6%)
  starting transfers between devices  17.2 us (4%)
  between operations  14.3 us (3%)
  other arithmetic  10.8 us (3%)
  local copies, waits for them, and re-layouts  4.89 us (1%)
    psum x3, blocking collectives, group_norm(): sums = lax.psum(jnp.sum(grouped, axis=(0, 2)), ('tile', 'head'))  122 us
    psum x3, blocking collectives, group_norm(): lax.psum(jnp.sum(deviation * deviation, axis=(0, 2)), ('tile', 'head'))  121 us
    all_gather x1, waiting for transfers between devices, per_device(): key_rows = lax.all_gather(keys, 'tile', axis=0, tiled=True)  29.1 us
    all_gather x1, waiting for transfers between devices, per_device(): tile_queries = lax.all_gather(queries, 'head', axis=0, tiled=True)  24.9 us
    reduce_scatter x1, waiting for transfers between devices, per_device(): lax.psum_scatter((weighted * factor[:, None]).astype(jnp.bfloat16), 'head...  15 us
    ppermute x4, waiting for transfers between devices, extended(): after = lax.ppermute(initial, axis, down)  13.3 us
    ppermute x4, starting transfers between devices, extended(): before = lax.ppermute(last, axis, up)  9.27 us
    unnamed x1, blocking collectives  9.13 us
  transfers between devices with their start and end apart: 12, of which 8 were waited for; matrix products, arithmetic and copies ran while one was open for 4% of the time, Pallas kernels for 0%

commit v1 on v0

v1 whole, which is shorter than its diff:
```python
import functools

import jax
import jax.numpy as jnp
from jax import lax
from jax.experimental import pallas as pl
from jax.experimental.pallas import tpu as pltpu
from jax.sharding import PartitionSpec as P

C = 512
GROUPS = 32
WIDTH = C // GROUPS
EPS = 1e-06
MESH = pl.DeviceIdType.MESH
VMEM = pl.BlockSpec(memory_space=pltpu.VMEM)


def moved(tile, head, tiles, heads, dt, dh):
    return (lax.rem(tile + dt + tiles, tiles), lax.rem(head + dh + heads, heads))


def all_barrier(tile, head, tiles, heads):
    total = tiles * heads
    me = tile * heads + head
    barrier = pltpu.get_barrier_semaphore()

    def greet(k, carry):
        peer = lax.rem(me + k, total)
        pl.semaphore_signal(
            barrier, inc=1, device_id=(peer // heads, lax.rem(peer, heads)), device_id_type=MESH
        )
        return carry

    lax.fori_loop(1, total, greet, 0)
    pl.semaphore_wait(barrier, total - 1)


def stats_copy(stat_ref, slots_ref, send, recv, me, total, heads, k):
    peer = lax.rem(me + k, total)
    return pltpu.make_async_remote_copy(
        src_ref=stat_ref,
        dst_ref=slots_ref.at[k],
        send_sem=send.at[k],
        recv_sem=recv.at[k],
        device_id=(peer // heads, lax.rem(peer, heads)),
        device_id_type=MESH,
    )


def exchange_kernel(tiles, heads, plan, npay, *refs):
    stat_ref, pays = refs[0], refs[1 : 1 + npay]
    slots_ref, gots = refs[1 + npay], refs[2 + npay : 2 + npay + len(plan)]
    s_send, s_recv, p_send, p_recv = refs[2 + npay + len(plan) :]
    total = tiles * heads
    tile, head = lax.axis_index("tile"), lax.axis_index("head")
    me = tile * heads + head
    all_barrier(tile, head, tiles, heads)
    copies = []
    for i, (src, dt, dh) in enumerate(plan):
        copies.append(
            pltpu.make_async_remote_copy(
                src_ref=pays[src],
                dst_ref=gots[i],
                send_sem=p_send.at[i],
                recv_sem=p_recv.at[i],
                device_id=moved(tile, head, tiles, heads, dt, dh),
                device_id_type=MESH,
            )
        )
    one = functools.partial(stats_copy, stat_ref, slots_ref, s_send, s_recv, me, total, heads)

    def begin(k, carry):
        one(k).start()
        return carry

    def finish(k, carry):
        one(k).wait()
        return carry

    lax.fori_loop(1, total, begin, 0)
    for copy in copies:
        copy.start()
    slots_ref[0] = stat_ref[...]
    lax.fori_loop(1, total, finish, 0)
    for copy in copies:
        copy.wait()


def exchange(cid, stat, payloads, plan):
    tiles, heads = lax.axis_size("tile"), lax.axis_size("head")
    total = tiles * heads
    outs = [jax.ShapeDtypeStruct((total, 1, 128), jnp.float32)]
    outs += [jax.ShapeDtypeStruct(payloads[s].shape, payloads[s].dtype) for s, _, _ in plan]
    return pl.pallas_call(
        functools.partial(exchange_kernel, tiles, heads, plan, len(payloads)),
        out_shape=outs,
        in_specs=[VMEM] * (1 + len(payloads)),
        out_specs=[VMEM] * len(outs),
        scratch_shapes=[
            pltpu.SemaphoreType.DMA((total,)),
            pltpu.SemaphoreType.DMA((total,)),
            pltpu.SemaphoreType.DMA((len(plan),)),
            pltpu.SemaphoreType.DMA((len(plan),)),
        ],
        compiler_params=pltpu.CompilerParams(collective_id=cid, has_side_effects=True),
        name="exchange_%d" % cid,
    )(stat, *payloads)


def gather_kernel(tiles, heads, stat_ref, res_ref, slots_ref, kv_ref, q_ref, *sems):
    s_send, s_recv, z_send, z_recv, c_send, c_recv, q_send, q_recv = sems
    total = tiles * heads
    tile, head = lax.axis_index("tile"), lax.axis_index("head")
    me = tile * heads + head
    partner = (tile + 1 - 2 * lax.rem(tile, 2), head)
    all_barrier(tile, head, tiles, heads)
    one = functools.partial(stats_copy, stat_ref, slots_ref, s_send, s_recv, me, total, heads)

    def begin(k, carry):
        one(k).start()
        return carry

    def finish(k, carry):
        one(k).wait()
        return carry

    lax.fori_loop(1, total, begin, 0)

    def zcopy(k):
        return pltpu.make_async_remote_copy(
            src_ref=res_ref,
            dst_ref=kv_ref.at[0, k],
            send_sem=z_send.at[k],
            recv_sem=z_recv.at[k],
            device_id=(tile, lax.rem(head + k, heads)),
            device_id_type=MESH,
        )

    def ccopy(k):
        return pltpu.make_async_remote_copy(
            src_ref=res_ref if k == 0 else kv_ref.at[0, k],
            dst_ref=kv_ref.at[1, k],
            send_sem=c_send.at[k],
            recv_sem=c_recv.at[k],
            device_id=partner,
            device_id_type=MESH,
        )

    def qcopy(j):
        return pltpu.make_async_remote_copy(
            src_ref=res_ref,
            dst_ref=q_ref.at[j],
            send_sem=q_send.at[j],
            recv_sem=q_recv.at[j],
            device_id=(lax.rem(tile + 2 * j, tiles), head),
            device_id_type=MESH,
        )

    for k in range(1, heads):
        zcopy(k).start()
    for j in range(1, tiles // 2):
        qcopy(j).start()
    ccopy(0).start()
    kv_ref[0, 0] = res_ref[...]
    q_ref[0] = res_ref[...]
    slots_ref[0] = stat_ref[...]
    lax.fori_loop(1, total, finish, 0)
    for k in range(1, heads):
        zcopy(k).wait_recv()
        ccopy(k).start()
    for k in range(1, heads):
        zcopy(k).wait_send()
    for j in range(1, tiles // 2):
        qcopy(j).wait()
    for k in range(heads):
        ccopy(k).wait()


def gather(cid, stat, resid):
    tiles, heads = lax.axis_size("tile"), lax.axis_size("head")
    total = tiles * heads
    n, c = resid.shape
    dma = pltpu.SemaphoreType.DMA
    return pl.pallas_call(
        functools.partial(gather_kernel, tiles, heads),
        out_shape=[
            jax.ShapeDtypeStruct((total, 1, 128), jnp.float32),
            jax.ShapeDtypeStruct((2, heads, n, c), resid.dtype),
            jax.ShapeDtypeStruct((tiles // 2, n, c), resid.dtype),
        ],
        in_specs=[VMEM] * 2,
        out_specs=[VMEM] * 3,
        scratch_shapes=[dma((total,))] * 2
        + [dma((heads,))] * 4
        + [dma((tiles // 2,))] * 2,

        compiler_params=pltpu.CompilerParams(collective_id=cid, has_side_effects=True),
        name="gather_%d" % cid,
    )(stat, resid)


def scatter_kernel(tiles, heads, o_ref, l_ref, og_ref, lg_ref, o_send, o_recv, l_send, l_recv):
    tile, head = lax.axis_index("tile"), lax.axis_index("head")
    half = tiles // 2
    barrier = pltpu.get_barrier_semaphore()
    for j in range(1, half):
        pl.semaphore_signal(
            barrier,
            inc=1,
            device_id=(lax.rem(tile + 2 * j, tiles), head),
            device_id_type=MESH,
        )
    pl.semaphore_wait(barrier, half - 1)
    copies = []
    for src, dst, send, recv in ((l_ref, lg_ref, l_send, l_recv), (o_ref, og_ref, o_send, o_recv)):
        for j in range(1, half):
            copies.append(
                pltpu.make_async_remote_copy(
                    src_ref=src.at[j],
                    dst_ref=dst.at[j],
                    send_sem=send.at[j],
                    recv_sem=recv.at[j],
                    device_id=(lax.rem(tile + tiles - 2 * j, tiles), head),
                    device_id_type=MESH,
                )
            )
    for copy in copies:
        copy.start()
    og_ref[0] = o_ref[0]
    lg_ref[0] = l_ref[0]
    for copy in copies:
        copy.wait()


def scatter(cid, outs, lse):
    tiles, heads = lax.axis_size("tile"), lax.axis_size("head")
    dma = pltpu.SemaphoreType.DMA((tiles // 2,))
    return pl.pallas_call(
        functools.partial(scatter_kernel, tiles, heads),
        out_shape=[
            jax.ShapeDtypeStruct(outs.shape, outs.dtype),
            jax.ShapeDtypeStruct(lse.shape, lse.dtype),
        ],
        in_specs=[VMEM] * 2,
        out_specs=[VMEM] * 2,
        scratch_shapes=[dma] * 4,
        compiler_params=pltpu.CompilerParams(collective_id=cid, has_side_effects=True),
        name="scatter_%d" % cid,
    )(outs, lse)


def spread(per_group):
    return jnp.broadcast_to(per_group[:, None], (GROUPS, WIDTH)).reshape(C)


def local_stats(flat):
    count = flat.shape[0] * WIDTH
    mean = jnp.sum(jnp.sum(flat, axis=0).reshape(GROUPS, WIDTH), axis=1) / count
    deviation = flat - spread(mean)
    square = jnp.sum(jnp.sum(deviation * deviation, axis=0).reshape(GROUPS, WIDTH), axis=1)
    pad = jnp.zeros((128 - 2 * GROUPS,), jnp.float32)
    return jnp.concatenate([mean, square, pad]).reshape(1, 128)


def combined(slots, count, gain, shift):
    total = slots.shape[0]
    means, squares = slots[:, 0, :GROUPS], slots[:, 0, GROUPS : 2 * GROUPS]
    mean = jnp.sum(means, axis=0) / total
    gap = means - mean[None]
    variance = (jnp.sum(squares, axis=0) + count * jnp.sum(gap * gap, axis=0)) / (total * count)
    return spread(mean), spread(lax.rsqrt(variance + EPS)) * gain, shift


def normalize(values, norm):
    mean, scale, shift = norm
    return (values - mean) * scale + shift


def conv(act, weight):
    return lax.conv_general_dilated(
        act[None],
        weight,
        (1, 1),
        "VALID",
        dimension_numbers=("NHWC", "HWIO", "NHWC"),
        preferred_element_type=jnp.float32,
    )[0]


def inside(rows, cols, first_row, first_col, all_rows, all_cols):
    r = first_row + lax.broadcasted_iota(jnp.int32, (rows, cols, 1), 0)
    c = first_col + lax.broadcasted_iota(jnp.int32, (rows, cols, 1), 1)
    return (r >= 0) & (r < all_rows) & (c >= 0) & (c < all_cols)


def per_device(
    latent,
    norm1_gain,
    norm1_shift,
    conv1_weight,
    conv1_bias,
    norm2_gain,
    norm2_shift,
    conv2_weight,
    conv2_bias,
    norm3_gain,
    norm3_shift,
    query_weight,
    query_bias,
    key_weight,
    value_weight,
    value_bias,
    out_weight,
    out_bias,
):
    rows, cols, channels = latent.shape
    tiles, heads = lax.axis_size("tile"), lax.axis_size("head")
    tile, head = lax.axis_index("tile"), lax.axis_index("head")
    n = rows * cols
    count = n * WIDTH
    latent32 = latent.astype(jnp.float32)

    top, bottom = latent[:2], latent[rows - 2 :]
    west, east = latent[:, 0], latent[:, cols - 1]
    payloads = [top, bottom, west, east, west[:2], east[:2], west[rows - 2 :], east[rows - 2 :]]
    plan = (
        (1, 1, 0),
        (0, -1, 0),
        (3, 0, 1),
        (2, 0, -1),
        (7, 1, 1),
        (6, 1, -1),
        (5, -1, 1),
        (4, -1, -1),
    )
    slots, above, below, left, right, al, ar, bl, br = exchange(
        1, local_stats(latent32.reshape(n, C)), payloads, plan
    )
    lefts = jnp.concatenate([al, left, bl], axis=0)[:, None]
    rights = jnp.concatenate([ar, right, br], axis=0)[:, None]
    middle = jnp.concatenate([above, latent, below], axis=0)
    wide = jnp.concatenate([lefts, middle, rights], axis=1).astype(jnp.float32)
    first_row, first_col = tile * rows, head * cols
    all_rows, all_cols = rows * tiles, cols * heads
    act1 = jax.nn.silu(normalize(wide, combined(slots, count, norm1_gain, norm1_shift)))
    mask1 = inside(rows + 4, cols + 2, first_row - 2, first_col - 1, all_rows, all_cols)
    act1 = jnp.where(mask1, act1, 0.0).astype(jnp.bfloat16)
    hidden = conv(act1, conv1_weight) + conv1_bias

    slots, left, right = exchange(
        2,
        local_stats(hidden[1 : rows + 1].reshape(n, C)),
        [hidden[:, 0], hidden[:, cols - 1]],
        ((1, 0, 1), (0, 0, -1)),
    )
    wide = jnp.concatenate([left[:, None], hidden, right[:, None]], axis=1)
    act2 = jax.nn.silu(normalize(wide, combined(slots, count, norm2_gain, norm2_shift)))
    mask2 = inside(rows + 2, cols + 2, first_row - 1, first_col - 1, all_rows, all_cols)
    act2 = jnp.where(mask2, act2, 0.0).astype(jnp.bfloat16)
    resid = (latent32 + (conv(act2, conv2_weight) + conv2_bias)).astype(jnp.bfloat16)
    resid = resid.reshape(n, C)

    slots, kv_res, q_res = gather(3, local_stats(resid.astype(jnp.float32)), resid)
    norm3 = combined(slots, count, norm3_gain, norm3_shift)
    kv_in = normalize(kv_res.reshape(-1, C).astype(jnp.float32), norm3).astype(jnp.bfloat16)
    q_in = normalize(q_res.reshape(-1, C).astype(jnp.float32), norm3).astype(jnp.bfloat16)
    queries = (jnp.dot(q_in, query_weight, preferred_element_type=jnp.float32) + query_bias).astype(
        jnp.bfloat16
    )
    keys = jnp.dot(kv_in, key_weight, preferred_element_type=jnp.float32).astype(jnp.bfloat16)
    values = (
        jnp.dot(kv_in, value_weight, preferred_element_type=jnp.float32) + value_bias
    ).astype(jnp.bfloat16)
    softmax_scale = 1.0 / C**0.5

    def attend(block):
        scores = jnp.dot(block, keys.T, preferred_element_type=jnp.float32) * softmax_scale
        peak = jnp.max(scores, axis=1)
        expo = jnp.exp(scores - peak[:, None])
        total = jnp.sum(expo, axis=1)
        weighted = jnp.dot(expo.astype(jnp.bfloat16), values, preferred_element_type=jnp.float32)
        return (weighted / total[:, None]).astype(jnp.bfloat16), peak + jnp.log(total)

    half = tiles // 2
    blocks = 4 if half % 4 == 0 else half
    if half == blocks:
        part, lse = attend(queries)
    else:
        part, lse = lax.map(attend, queries.reshape(half // blocks, blocks * n, C))
    got, got_lse = scatter(4, part.reshape(half, n, C), lse.reshape(half, n // 128, 128))
    got_lse = got_lse.reshape(half, n)
    weight = jnp.exp(got_lse - jnp.max(got_lse, axis=0))
    weight = weight / jnp.sum(weight, axis=0)
    attended = jnp.sum(weight[:, :, None] * got.astype(jnp.float32), axis=0).astype(jnp.bfloat16)
    mixed = (
        resid.astype(jnp.float32)
        + jnp.dot(attended, out_weight, preferred_element_type=jnp.float32)
        + out_bias
    )
    return mixed.astype(jnp.bfloat16).reshape(rows, cols, C)


def solution(mesh):
    return jax.shard_map(
        per_device,
        mesh=mesh,
        in_specs=(P("tile", "head", None),) + (P(),) * 17,
        out_specs=P("tile", "head", None),
        check_vma=False,
    )
```

time: 430 us -> 159 us (0.37)
  blocking collectives: 262 us -> 0 us
  waiting for transfers between devices: 91.3 us -> 0 us
  Pallas kernels: 0 us -> 74.2 us
  matrix products: 25.3 us -> 53 us
  starting transfers between devices: 17.2 us -> 0 us
  between operations: 14.3 us -> 0.38 us
  other arithmetic: 10.8 us -> 24.7 us
    psum x6 -> x0, blocking collectives: 244 us -> none  [the longest x3 122 us: group_norm(): sums = lax.psum(jnp.sum(grouped, axis=(0, 2)), ('tile', 'head'))]
    pallas_call x0 -> x4, Pallas kernels: none -> 74.2 us  [the longest x1 32.6 us: gather(): pl.pallas_call(functools.partial(gather_kernel, tiles, heads), out_shape=...]
    all_gather x3 -> x0, waiting for transfers between devices: 63 us -> none  [the longest x1 29.1 us: per_device(): key_rows = lax.all_gather(keys, 'tile', axis=0, tiled=True)]
    conv_general_dilated x2, matrix products: 5.31 us -> 34.4 us  [conv(): lax.conv_general_dilated(act[None], weight, (1, 1), 'VALID', dimension_nu...]
    ppermute x8 -> x0, starting transfers between devices: 17.1 us -> none  [the longest x4 9.27 us: extended(): before = lax.ppermute(last, axis, up)]
    reduce_scatter x1 -> x0, waiting for transfers between devices: 15 us -> none  [per_device(): lax.psum_scatter((weighted * factor[:, None]).astype(jnp.bfloat16), 'head...]
    ppermute x8 -> x0, waiting for transfers between devices: 13.3 us -> none  [the longest x4 13.3 us: extended(): after = lax.ppermute(initial, axis, down)]
    unnamed x1 -> x0, blocking collectives: 9.13 us -> none
  transfers between devices with their start and end apart: 12 -> 0, of which waited for: 8 -> 0; matrix products, arithmetic and copies ran while one was open for 4% -> 0% of each run, Pallas kernels for 0% -> 0%
where the time goes in v1:
time: 159 us; the launch traced here: 158 us
  Pallas kernels  74.2 us (47%)
  matrix products  53 us (33%)
  other arithmetic  24.7 us (16%)
  local copies, waits for them, and re-layouts  5.31 us (3%)
    conv_general_dilated x2, matrix products, conv(): lax.conv_general_dilated(act[None], weight, (1, 1), 'VALID', dimension_nu...  34.4 us
    pallas_call x1, Pallas kernels, gather(): pl.pallas_call(functools.partial(gather_kernel, tiles, heads), out_shape=...  32.6 us
    pallas_call x2, Pallas kernels, exchange(): pl.pallas_call(functools.partial(exchange_kernel, tiles, heads, plan, len...  24 us
    pallas_call x1, Pallas kernels, scatter(): pl.pallas_call(functools.partial(scatter_kernel, tiles, heads), out_shape...  17.6 us
    dot_general x1, matrix products, attend(): jnp.dot(expo.astype(jnp.bfloat16), values, preferred_element_type=jnp.flo...  7.9 us
    dot_general x1, matrix products, attend(): jnp.dot(block, keys.T, preferred_element_type=jnp.float32) * softmax_scale  7.87 us
    reduce_sum x1, other arithmetic, attend(): total = jnp.sum(expo, axis=1)  4.61 us

profile of v1, /device:TPU:8, one launch (start us, length us, event | category | flops | bytes accessed | tf_op | source)
XLA Modules:
  0.0 157.6 jit_solution(7832939643939842618)
XLA Ops:
  0.2 1.0 convert_reduce_fusion
  1.2 0.7 fusion.54
  2.0 0.6 copy_bitcast_fusion
  2.6 0.1 reduce_sum.217
  2.8 0.1 sub.149
  2.9 1.1 fusion.39
  4.1 0.1 reduce_sum.219
  4.2 0.6 fusion.46.refs_0_
  4.8 14.3 %exchange_1.1 = (f32[32,1,128]{2,1,0:T(1,128)}, bf16[2,128,512]{2,1,0:T(8,128)(2,1)}, bf16[2,128,512]{2,1,0:T(8,128)(2,1)}, bf16[2,512]{1,0:T(2,128)(2,1)}, bf16...) custom-call(f32[1,128]{1,0:T(1,128)} %fusion.46.refs_0_, ...), custom_call_target="tpu_custom_call" | custom-call | tf_op jit(solution)/shard_map/exchange_1/pallas_call | solution.py:94
  19.1 0.7 maximum_bitcast_fusion.1
  19.8 0.7 maximum_bitcast_fusion.2
  20.5 0.9 slice_reduce_fusion.6
  21.6 0.1 reshape.420
  21.7 0.7 mul.144
  22.5 1.2 maximum_bitcast_fusion
  23.7 0.8 select_convert_fusion
  24.5 19.8 %broadcast_add_fusion = (f32[1,4,128,512]{3,0,2,1:T(1,128)S(1)}, f32[1,4,128,512]{3,0,2,1:T(1,128)S(1)}) fusion(f32[512]{0:T(512)S(1)} %copy-done.6, bf16[3,3,512,512]{3,2,1,0:T(8,128)(2,1)} %param.21, bf16[1,6,130,512]{3,2,1,0:T(8,128)(2,1)S(1)} %select_convert_fusion), kind=kOutput, calls=%fused_computation.57 | convolution fusion | flops 2416181248 | bytes 7616512 | tf_op jit(solution)/shard_map/conv_general_dilated | solution.py:280
  44.4 0.7 bitcast_add_fusion
  45.1 0.3 slice_reduce_fusion
  45.5 0.1 reduce_sum.224
  45.8 0.5 multiply_reduce_fusion.2
  46.2 0.6 slice_bitcast_fusion
  46.9 0.1 reduce_sum.226
  47.0 0.6 fusion.47.refs_0_
  47.7 9.7 %exchange_2.1 = (f32[32,1,128]{2,1,0:T(1,128)}, f32[4,512]{1,0:T(4,128)}, f32[4,512]{1,0:T(4,128)}) custom-call(f32[1,128]{1,0:T(1,128)} %fusion.47.refs_0_, f32[4,512]{1,0:T(4,128)} %get-tuple-element.48.refs_1_, f32[4,512]{1,0:T(4,128)} %get-tuple-element.47.refs_2_), custom_call_target="tpu_custom_call" | custom-call | tf_op jit(solution)/shard_map/exchange_2/pallas_call | solution.py:94
  57.4 0.7 copy.33
  58.1 0.7 copy.34
  58.8 0.9 slice_reduce_fusion.5
  60.2 14.6 %fusion.19 = f32[1,2,128,512]{3,0,2,1:T(1,128)S(1)} fusion(bf16[3,3,512,512]{3,2,1,0:T(8,128)(2,1)} %param.25, pred[4,130]{1,0:T(4,128)(4,1)S(1)} %and_and_fusion.1, f32[1,4,1,512]{3,0,2,1:T(1,128)S(1)} %copy.34, f32[1,4,128,512]{3,0,2,1:T(1,128)S(1)} %get-tuple-element.54, f32[1,4,1,512]{3,0,2,1:T(1,128)S(1)} %copy.33, f32[512]{0:T(512)S(1)} %copy-done.15, ...), kind=kOutput, calls=%fused_computation.29 | convolution fusion | flops 1210888192 | bytes 6314504 | tf_op jit(solution)/shard_map/conv_general_dilated | solution.py:280
  74.8 0.1 convert_reduce_fusion.1
  75.0 0.1 reduce_sum.231
  75.2 0.1 fusion.37
  75.4 0.1 reduce_sum.233
  75.5 0.6 fusion.48.stat_ref
  76.2 32.6 %gather_3.1 = (f32[32,1,128]{2,1,0:T(1,128)}, bf16[2,4,256,512]{3,2,1,0:T(8,128)(2,1)}, bf16[4,256,512]{2,1,0:T(8,128)(2,1)}) custom-call(f32[1,128]{1,0:T(1,128)} %fusion.48.stat_ref, bf16[256,512]{1,0:T(8,128)(2,1)} %bitcast.60), custom_call_target="tpu_custom_call" | custom-call | tf_op jit(solution)/shard_map/gather_3/pallas_call | solution.py:184
  108.8 0.9 slice_reduce_fusion.4
  110.1 2.4 %fusion.6 = bf16[2048,512]{1,0:T(8,128)(2,1)S(1)} fusion(bf16[2,4,256,512]{3,2,1,0:T(8,128)(2,1)} %get-tuple-element.36, f32[512]{0:T(512)S(1)} %copy-done.8, f32[512]{0:T(512)S(1)} %mul.158, f32[512]{0:T(512)S(1)} %sub.168), kind=kLoop, calls=%fused_computation.8 | loop fusion | flops 5242880 | bytes 4200448 | tf_op jit(solution)/shard_map/convert_element_type | solution.py:365
  112.5 1.8 %add_convert_fusion.1 = bf16[1024,512]{1,0:T(8,128)(2,1)} fusion(bf16[512,512]{1,0:T(8,128)(2,1)S(1)} %copy-done.13, bf16[1024,512]{1,0:T(8,128)(2,1)S(1)} %bitcast.72, f32[512]{0:T(512)S(1)} %copy-done.16, f32[512]{0:T(512)S(1)} %copy-done.8, f32[512]{0:T(512)S(1)} %mul.158, f32[512]{0:T(512)S(1)} %sub.168), kind=kOutput, calls=%fused_computation.20 | convolution fusion | flops 540540928 | bytes 2629632 | tf_op jit(solution)/shard_map/dot_general | solution.py:367
  114.3 7.9 %multiply_reduce_fusion = (f32[1024]{0:T(1024)S(1)}, f32[1024,2048]{1,0:T(8,128)}) fusion(bf16[1024,512]{1,0:T(8,128)(2,1)} %add_convert_fusion.1, bf16[2048,512]{1,0:T(8,128)(2,1)S(1)} %fusion.6, bf16[512,512]{1,0:T(8,128)(2,1)S(1)} %copy-done), kind=kOutput, calls=%fused_computation.1 | convolution fusion | flops 3226467328 | bytes 12062720 | tf_op jit(solution)/shard_map/dot_general | solution.py:377
  122.2 4.6 %fusion = f32[1024]{0:T(1024)S(1)} fusion(f32[1024,2048]{1,0:T(8,128)} %get-tuple-element.57, f32[1024]{0:T(1024)S(1)} %get-tuple-element.56), kind=kLoop, calls=%fused_computation.2 | loop fusion | flops 6290432 | bytes 8396800 | tf_op jit(solution)/shard_map/reduce_sum | solution.py:380
  126.8 7.9 %divide_convert_fusion = bf16[1024,512]{1,0:T(8,128)(2,1)} fusion(f32[1024,2048]{1,0:T(8,128)} %get-tuple-element.57, f32[1024]{0:T(1024)S(1)} %get-tuple-element.56, f32[1024]{0:T(1024)S(1)} %fusion, bf16[2048,512]{1,0:T(8,128)(2,1)S(1)} %fusion.6, bf16[512,512]{1,0:T(8,128)(2,1)S(1)} %copy-done.14, f32[512]{0:T(512)S(1)} %copy-done.17), kind=kOutput, calls=%fused_computation.19 | convolution fusion | flops 3230662656 | bytes 12068864 | tf_op jit(solution)/shard_map/dot_general | solution.py:381
  134.7 0.6 log_add_fusion
  135.3 17.6 %scatter_4.1 = (bf16[4,256,512]{2,1,0:T(8,128)(2,1)}, f32[4,2,128]{2,1,0:T(2,128)}) custom-call(bf16[4,256,512]{2,1,0:T(8,128)(2,1)} %bitcast.62, f32[4,2,128]{2,1,0:T(2,128)} %bitcast.67), custom_call_target="tpu_custom_call" | custom-call | tf_op jit(solution)/shard_map/scatter_4/pallas_call | solution.py:238
  152.9 0.7 reduce_max.19
  153.6 0.7 exponential_reduce_fusion
  154.3 0.7 fusion.43
  155.0 1.5 multiply_reduce_fusion.1
  156.5 1.0 fusion.17
  (80 shorter events, 2.1 us)
Async XLA Ops:
  0.0 114.3 %copy-start = (bf16[512,512]{1,0:T(8,128)(2,1)S(1)}, bf16[512,512]{1,0:T(8,128)(2,1)}, u32[]{:S(2)}) copy-start(bf16[512,512]{1,0:T(8,128)(2,1)} %param.31) | copy-start | bytes 1572868
  0.0 23.7 %copy-start.5 = (f32[512]{0:T(512)S(1)}, f32[512]{0:T(512)}, u32[]{:S(2)}) copy-start(f32[512]{0:T(512)} %param.20) | copy-start | bytes 6148
  2.9 21.6 %copy-start.6 = (f32[512]{0:T(512)S(1)}, f32[512]{0:T(512)}, u32[]{:S(2)}) copy-start(f32[512]{0:T(512)} %param.22) | copy-start | bytes 6148
  44.4 15.6 %copy-start.10 = (f32[512]{0:T(512)S(1)}, f32[512]{0:T(512)}, u32[]{:S(2)}) copy-start(f32[512]{0:T(512)} %param.23) | copy-start | bytes 6148
  44.4 15.7 %copy-start.15 = (f32[512]{0:T(512)S(1)}, f32[512]{0:T(512)}, u32[]{:S(2)}) copy-start(f32[512]{0:T(512)} %param.24) | copy-start | bytes 6148
  60.1 14.6 %copy-start.1 = (bf16[2,128,512]{2,1,0:T(8,128)(2,1)S(1)}, bf16[2,128,512]{2,1,0:T(8,128)(2,1)}, u32[]{:S(2)}) copy-start(bf16[2,128,512]{2,1,0:T(8,128)(2,1)} %refs_2_.1) | copy-start | bytes 786436
  60.1 14.6 %copy-start.7 = (f32[512]{0:T(512)S(1)}, f32[512]{0:T(512)}, u32[]{:S(2)}) copy-start(f32[512]{0:T(512)} %param.26) | copy-start | bytes 6148
  60.1 49.7 %copy-start.11 = (f32[512]{0:T(512)S(1)}, f32[512]{0:T(512)}, u32[]{:S(2)}) copy-start(f32[512]{0:T(512)} %param.27) | copy-start | bytes 6148
  60.2 49.9 %copy-start.8 = (f32[512]{0:T(512)S(1)}, f32[512]{0:T(512)}, u32[]{:S(2)}) copy-start(f32[512]{0:T(512)} %param.28) | copy-start | bytes 6148
  74.9 1.3 copy-start.2
  110.0 2.4 %copy-start.12 = (bf16[4,256,512]{2,1,0:T(8,128)(2,1)S(1)}, bf16[4,256,512]{2,1,0:T(8,128)(2,1)}, u32[]{:S(2)}) copy-start(bf16[4,256,512]{2,1,0:T(8,128)(2,1)} %get-tuple-element.34) | copy-start | bytes 3145732
  110.0 2.4 %copy-start.13 = (bf16[512,512]{1,0:T(8,128)(2,1)S(1)}, bf16[512,512]{1,0:T(8,128)(2,1)}, u32[]{:S(2)}) copy-start(bf16[512,512]{1,0:T(8,128)(2,1)} %param.29) | copy-start | bytes 1572868
  110.1 2.4 %copy-start.16 = (f32[512]{0:T(512)S(1)}, f32[512]{0:T(512)}, u32[]{:S(2)}) copy-start(f32[512]{0:T(512)} %param.30) | copy-start | bytes 6148
  122.2 4.6 %copy-start.14 = (bf16[512,512]{1,0:T(8,128)(2,1)S(1)}, bf16[512,512]{1,0:T(8,128)(2,1)}, u32[]{:S(2)}) copy-start(bf16[512,512]{1,0:T(8,128)(2,1)} %param.32) | copy-start | bytes 1572868
  122.2 4.6 %copy-start.17 = (f32[512]{0:T(512)S(1)}, f32[512]{0:T(512)}, u32[]{:S(2)}) copy-start(f32[512]{0:T(512)} %param.33) | copy-start | bytes 6148
  134.7 21.8 %copy-start.3 = (bf16[2,128,512]{2,1,0:T(8,128)(2,1)S(1)}, bf16[2,128,512]{2,1,0:T(8,128)(2,1)}, u32[]{:S(2)}) copy-start(bf16[2,128,512]{2,1,0:T(8,128)(2,1)} %copy-done.2) | copy-start | bytes 786436
  134.7 21.8 %copy-start.4 = (bf16[512,512]{1,0:T(8,128)(2,1)S(1)}, bf16[512,512]{1,0:T(8,128)(2,1)}, u32[]{:S(2)}) copy-start(bf16[512,512]{1,0:T(8,128)(2,1)} %param.34) | copy-start | bytes 1572868
  134.7 21.8 %copy-start.9 = (f32[512]{0:T(512)S(1)}, f32[512]{0:T(512)}, u32[]{:S(2)}) copy-start(f32[512]{0:T(512)} %param.35) | copy-start | bytes 6148

commit v2 on v1

--- a/solution.py
+++ b/solution.py
@@ -199,9 +199,28 @@
     )(stat, resid)
 
 
-def scatter_kernel(tiles, heads, o_ref, l_ref, og_ref, lg_ref, o_send, o_recv, l_send, l_recv):
+def attend_kernel(
+    tiles,
+    heads,
+    q_ref,
+    k_ref,
+    v_ref,
+    res_ref,
+    w_ref,
+    b_ref,
+    out_ref,
+    o_scr,
+    og_scr,
+    l_scr,
+    lg_scr,
+    o_send,
+    o_recv,
+    l_send,
+    l_recv,
+):
     tile, head = lax.axis_index("tile"), lax.axis_index("head")
     half = tiles // 2
+    n = res_ref.shape[0]
     barrier = pltpu.get_barrier_semaphore()
     for j in range(1, half):
         pl.semaphore_signal(
@@ -211,42 +230,115 @@
             device_id_type=MESH,
         )
     pl.semaphore_wait(barrier, half - 1)
-    copies = []
-    for src, dst, send, recv in ((l_ref, lg_ref, l_send, l_recv), (o_ref, og_ref, o_send, o_recv)):
-        for j in range(1, half):
-            copies.append(
-                pltpu.make_async_remote_copy(
-                    src_ref=src.at[j],
-                    dst_ref=dst.at[j],
-                    send_sem=send.at[j],
-                    recv_sem=recv.at[j],
-                    device_id=(lax.rem(tile + tiles - 2 * j, tiles), head),
-                    device_id_type=MESH,
-                )
+    softmax_scale = 1.0 / C**0.5
+
+    def copies(j):
+        owner = (lax.rem(tile + tiles - 2 * j, tiles), head)
+        return [
+            pltpu.make_async_remote_copy(
+                src_ref=src.at[j],
+                dst_ref=dst.at[j],
+                send_sem=send.at[j],
+                recv_sem=recv.at[j],
+                device_id=owner,
+                device_id_type=MESH,
             )
-    for copy in copies:
-        copy.start()
-    og_ref[0] = o_ref[0]
-    lg_ref[0] = l_ref[0]
-    for copy in copies:
-        copy.wait()
-
-
-def scatter(cid, outs, lse):
+            for src, dst, send, recv in (
+                (o_scr, og_scr, o_send, o_recv),
+                (l_scr, lg_scr, l_send, l_recv),
+            )
+        ]
+
+    def compute(j, o_to, l_to):
+        scores = jnp.dot(q_ref[j], k_ref[...], preferred_element_type=jnp.float32) * softmax_scale
+        peak = jnp.max(scores, axis=1, keepdims=True)
+        expo = jnp.exp(scores - peak)
+        total = jnp.sum(expo, axis=1, keepdims=True)
+        weighted = jnp.dot(expo.astype(jnp.bfloat16), v_ref[...], preferred_element_type=jnp.float32)
+        lse = jnp.broadcast_to(peak + jnp.log(total), (n, 128))
+        l_to[j] = jnp.transpose(lse)[:8]
+        o_to[j] = (weighted / total).astype(jnp.bfloat16)
+
+    def step(j, carry):
+        compute(j, o_scr, l_scr)
+        for copy in copies(j):
+            copy.start()
+        return carry
+
+    lax.fori_loop(1, half, step, 0)
+    compute(0, og_scr, lg_scr)
+    for j in range(1, half):
+        for copy in copies(j):
+            copy.wait()
+    peak = lg_scr[0]
+    for j in range(1, half):
+        peak = jnp.maximum(peak, lg_scr[j])
+    weights = [jnp.exp(lg_scr[j] - peak) for j in range(half)]
+    total = weights[0]
+    for j in range(1, half):
+        total = total + weights[j]
+    mixed = jnp.zeros((n, C), jnp.float32)
+    for j in range(half):
+        column = jnp.transpose(jnp.broadcast_to((weights[j] / total)[:1], (128, n)))[:, :1]
+        mixed = mixed + column * og_scr[j].astype(jnp.float32)
+    out = jnp.dot(mixed.astype(jnp.bfloat16), w_ref[...], preferred_element_type=jnp.float32)
+    out_ref[...] = (res_ref[...].astype(jnp.float32) + out + b_ref[...]).astype(jnp.bfloat16)
+
+
+def attend(cid, queries, keys, values, resid, weight, bias):
     tiles, heads = lax.axis_size("tile"), lax.axis_size("head")
-    dma = pltpu.SemaphoreType.DMA((tiles // 2,))
+    half = tiles // 2
+    n = resid.shape[0]
+    dma = pltpu.SemaphoreType.DMA((half,))
     return pl.pallas_call(
-        functools.partial(scatter_kernel, tiles, heads),
-        out_shape=[
-            jax.ShapeDtypeStruct(outs.shape, outs.dtype),
-            jax.ShapeDtypeStruct(lse.shape, lse.dtype),
+        functools.partial(attend_kernel, tiles, heads),
+        out_shape=jax.ShapeDtypeStruct(resid.shape, resid.dtype),
+        in_specs=[VMEM] * 6,
+        out_specs=VMEM,
+        scratch_shapes=[pltpu.VMEM((half, n, C), jnp.bfloat16)] * 2
+        + [pltpu.VMEM((half, 8, n), jnp.float32)] * 2
+        + [dma] * 4,
+        compiler_params=pltpu.CompilerParams(collective_id=cid, has_side_effects=True),
+        name="attend_%d" % cid,
+    )(queries, keys, values, resid, weight, bias)
+
+
+def conv_kernel(act_ref, w_ref, b_ref, out_ref, lhs):
+    rows, cols = act_ref.shape[0] - 2, act_ref.shape[1] - 2
+
+    @pl.when(pl.program_id(0) == 0)
+    def unfold():
+        for dj in range(3):
+            moved_cols = act_ref[:, dj : dj + cols, :]
+            for di in range(3):
+                tap = 3 * di + dj
+                lhs[:, tap * C : (tap + 1) * C] = moved_cols[di : di + rows].reshape(rows * cols, C)
+
+    out_ref[...] = (
+        jnp.dot(lhs[...], w_ref[...], preferred_element_type=jnp.float32) + b_ref[...]
+    )
+
+
+def conv(act, weight, bias):
+    rows, cols = act.shape[0] - 2, act.shape[1] - 2
+    part = C // 2
+    out = pl.pallas_call(
+        conv_kernel,
+        grid=(C // part,),
+        out_shape=jax.ShapeDtypeStruct((rows * cols, C), jnp.float32),
+        in_specs=[
+            pl.BlockSpec(act.shape, lambda i: (0, 0, 0)),
+            pl.BlockSpec((9 * C, part), lambda i: (0, i)),
+            pl.BlockSpec((1, part), lambda i: (0, i)),
         ],
-        in_specs=[VMEM] * 2,
-        out_specs=[VMEM] * 2,
-        scratch_shapes=[dma] * 4,
-        compiler_params=pltpu.CompilerParams(collective_id=cid, has_side_effects=True),
-        name="scatter_%d" % cid,
-    )(outs, lse)
+        out_specs=pl.BlockSpec((rows * cols, part), lambda i: (0, i)),
+        scratch_shapes=[pltpu.VMEM((rows * cols, 9 * C), jnp.bfloat16)],
+        cost_estimate=pl.CostEstimate(
+            flops=2 * rows * cols * 9 * C * C, bytes_accessed=18 * C * C, transcendentals=0
+        ),
+        name="conv_%d" % rows,
+    )(act, weight.reshape(9 * C, C), bias.reshape(1, C))
+    return out.reshape(rows, cols, C)
 
 
 def spread(per_group):
@@ -274,17 +366,6 @@
 def normalize(values, norm):
     mean, scale, shift = norm
     return (values - mean) * scale + shift
-
-
-def conv(act, weight):
-    return lax.conv_general_dilated(
-        act[None],
-        weight,
-        (1, 1),
-        "VALID",
-        dimension_numbers=("NHWC", "HWIO", "NHWC"),
-        preferred_element_type=jnp.float32,
-    )[0]
 
 
 def inside(rows, cols, first_row, first_col, all_rows, all_cols):
@@ -345,7 +426,7 @@
     act1 = jax.nn.silu(normalize(wide, combined(slots, count, norm1_gain, norm1_shift)))
     mask1 = inside(rows + 4, cols + 2, first_row - 2, first_col - 1, all_rows, all_cols)
     act1 = jnp.where(mask1, act1, 0.0).astype(jnp.bfloat16)
-    hidden = conv(act1, conv1_weight) + conv1_bias
+    hidden = conv(act1, conv1_weight, conv1_bias)
 
     slots, left, right = exchange(
         2,
@@ -357,7 +438,7 @@
     act2 = jax.nn.silu(normalize(wide, combined(slots, count, norm2_gain, norm2_shift)))
     mask2 = inside(rows + 2, cols + 2, first_row - 1, first_col - 1, all_rows, all_cols)
     act2 = jnp.where(mask2, act2, 0.0).astype(jnp.bfloat16)
-    resid = (latent32 + (conv(act2, conv2_weight) + conv2_bias)).astype(jnp.bfloat16)
+    resid = (latent32 + conv(act2, conv2_weight, conv2_bias)).astype(jnp.bfloat16)
     resid = resid.reshape(n, C)
 
     slots, kv_res, q_res = gather(3, local_stats(resid.astype(jnp.float32)), resid)
@@ -367,37 +448,16 @@
     queries = (jnp.dot(q_in, query_weight, preferred_element_type=jnp.float32) + query_bias).astype(
         jnp.bfloat16
     )
-    keys = jnp.dot(kv_in, key_weight, preferred_element_type=jnp.float32).astype(jnp.bfloat16)
+    keys = lax.dot_general(
+        key_weight, kv_in, (((0,), (1,)), ((), ())), preferred_element_type=jnp.float32
+    ).astype(jnp.bfloat16)
     values = (
         jnp.dot(kv_in, value_weight, preferred_element_type=jnp.float32) + value_bias
     ).astype(jnp.bfloat16)
-    softmax_scale = 1.0 / C**0.5
-
-    def attend(block):
-        scores = jnp.dot(block, keys.T, preferred_element_type=jnp.float32) * softmax_scale
-        peak = jnp.max(scores, axis=1)
-        expo = jnp.exp(scores - peak[:, None])
-        total = jnp.sum(expo, axis=1)
-        weighted = jnp.dot(expo.astype(jnp.bfloat16), values, preferred_element_type=jnp.float32)
-        return (weighted / total[:, None]).astype(jnp.bfloat16), peak + jnp.log(total)
-
-    half = tiles // 2
-    blocks = 4 if half % 4 == 0 else half
-    if half == blocks:
-        part, lse = attend(queries)
-    else:
-        part, lse = lax.map(attend, queries.reshape(half // blocks, blocks * n, C))
-    got, got_lse = scatter(4, part.reshape(half, n, C), lse.reshape(half, n // 128, 128))
-    got_lse = got_lse.reshape(half, n)
-    weight = jnp.exp(got_lse - jnp.max(got_lse, axis=0))
-    weight = weight / jnp.sum(weight, axis=0)
-    attended = jnp.sum(weight[:, :, None] * got.astype(jnp.float32), axis=0).astype(jnp.bfloat16)
-    mixed = (
-        resid.astype(jnp.float32)
-        + jnp.dot(attended, out_weight, preferred_element_type=jnp.float32)
-        + out_bias
-    )
-    return mixed.astype(jnp.bfloat16).reshape(rows, cols, C)
+    mixed = attend(
+        4, queries.reshape(-1, n, C), keys, values, resid, out_weight, out_bias.reshape(1, C)
+    )
+    return mixed.reshape(rows, cols, C)
 
 
 def solution(mesh):

time: 159 us -> 126 us (0.79)
  matrix products: 53 us -> 6.97 us
  Pallas kernels: 74.2 us -> 90 us
  other arithmetic: 24.7 us -> 19.7 us
  local copies, waits for them, and re-layouts: 5.31 us -> 8.43 us
    conv_general_dilated x2 -> x0, matrix products: 34.4 us -> none  [conv(): lax.conv_general_dilated(act[None], weight, (1, 1), 'VALID', dimension_nu...]
    pallas_call x1 -> x3, Pallas kernels: 17.6 us -> 33.4 us  [the longest x1 23.1 us: attend(): pl.pallas_call(functools.partial(attend_kernel, tiles, heads), out_shape=...]
    dot_general x3 -> x2, matrix products: 16.8 us -> 5.26 us  [the longest x1 2.68 us: per_device(): lax.dot_general(key_weight, kv_in, (((0,), (1,)), ((), ())), preferred_el...]
    reduce_sum x3 -> x0, other arithmetic: 6.84 us -> none  [the longest x1 4.61 us: attend(): total = jnp.sum(expo, axis=1)]
    unnamed x36 -> x29, local copies, waits for them, and re-layouts: 0.09 us -> 2.93 us
    concatenate x3 -> x0, other arithmetic: 2.6 us -> none  [per_device(): wide = jnp.concatenate([lefts, middle, rights], axis=1).astype(jnp.float32)]
    convert_element_type x1, other arithmetic: 0.79 us -> 2.74 us  [per_device(): act1 = jnp.where(mask1, act1, 0.0).astype(jnp.bfloat16)]
    reduce_sum x6, other arithmetic: 1.82 us -> 3.71 us  [local_stats(): mean = jnp.sum(jnp.sum(flat, axis=0).reshape(GROUPS, WIDTH), axis=1) / count]
where the time goes in v2:
time: 126 us; the launch traced here: 125 us
  Pallas kernels  90 us (71%)
  other arithmetic  19.7 us (16%)
  local copies, waits for them, and re-layouts  8.43 us (7%)
  matrix products  6.97 us (6%)
    pallas_call x1, Pallas kernels, gather(): pl.pallas_call(functools.partial(gather_kernel, tiles, heads), out_shape=...  32.6 us
    pallas_call x2, Pallas kernels, exchange(): pl.pallas_call(functools.partial(exchange_kernel, tiles, heads, plan, len...  24 us
    pallas_call x1, Pallas kernels, attend(): pl.pallas_call(functools.partial(attend_kernel, tiles, heads), out_shape=...  23.1 us
    pallas_call x2, Pallas kernels, conv(): pl.pallas_call(conv_kernel, grid=(C // part,), out_shape=jax.ShapeDtypeSt...  10.3 us
    reduce_sum x6, other arithmetic, local_stats(): mean = jnp.sum(jnp.sum(flat, axis=0).reshape(GROUPS, WIDTH), axis=1) / count  3.71 us
    unnamed x29, local copies, waits for them, and re-layouts  2.93 us
    convert_element_type x1, other arithmetic, per_device(): act1 = jnp.where(mask1, act1, 0.0).astype(jnp.bfloat16)  2.74 us
    reduce_sum x3, other arithmetic, combined(): mean = jnp.sum(means, axis=0) / total  2.74 us

profile of v2, /device:TPU:8, one launch (start us, length us, event | category | flops | bytes accessed | tf_op | source)
XLA Modules:
  0.0 125.2 jit_solution(11441069808477379579)
XLA Ops:
  0.2 1.0 convert_reduce_fusion
  1.2 0.7 fusion.25
  2.0 0.6 copy_bitcast_fusion.2
  2.6 0.1 reduce_sum.190
  2.8 0.1 sub.107
  2.9 1.1 fusion.16
  4.0 0.1 reduce_sum.192
  4.2 0.6 fusion.20.refs_0_
  4.8 14.3 %exchange_1.1 = (f32[32,1,128]{2,1,0:T(1,128)}, bf16[2,128,512]{2,1,0:T(8,128)(2,1)}, bf16[2,128,512]{2,1,0:T(8,128)(2,1)}, bf16[2,512]{1,0:T(2,128)(2,1)}, bf16...) custom-call(f32[1,128]{1,0:T(1,128)} %fusion.20.refs_0_, ...), custom_call_target="tpu_custom_call" | custom-call | tf_op jit(solution)/shard_map/exchange_1/pallas_call | solution.py:94
  19.0 0.7 maximum_bitcast_fusion
  19.8 0.7 maximum_bitcast_fusion.1
  20.5 0.9 slice_reduce_fusion.6
  21.5 0.1 reshape.239
  21.6 0.7 mul.101
  22.4 0.1 sub.110
  22.4 2.7 %select_convert_fusion.act_ref = bf16[6,130,512]{2,1,0:T(8,128)(2,1)} fusion(bf16[6,1,512]{2,1,0:T(2,128)(2,1)S(1)} %copy.25, bf16[2,128,512]{2,1,0:T(8,128)(2,1)} %get-tuple-element.24, bf16[2,128,512]{2,1,0:T(8,128)(2,1)S(1)} %copy-done.1, bf16[2,128,512]{2,1,0:T(8,128)(2,1)} %get-tuple-element.23, bf16[6,1,512]{2,1,0:T(2,128)(2,1)S(1)} %copy.24, ...), kind=kLoop, calls=%fused_computation.12 | loop fusion | flops 7587840 | bytes 1604364 | tf_op jit(solution)/shard_map/convert_element_type | solution.py:428
  25.2 6.0 %conv_4.1 = f32[512,512]{1,0:T(8,128)} custom-call(bf16[6,130,512]{2,1,0:T(8,128)(2,1)} %select_convert_fusion.act_ref, bf16[4608,512]{1,0:T(8,128)(2,1)} %bitcast.60, f32[1,512]{1,0:T(1,128)} %bitcast.62), custom_call_target="tpu_custom_call" | custom-call | flops 2415919104 | bytes 4718592 | tf_op jit(solution)/shard_map/conv_4/pallas_call | solution.py:325
  31.2 1.2 slice_reduce_fusion
  32.4 0.1 reduce_sum.197
  32.6 0.1 sub.115
  32.7 1.1 multiply_reduce_fusion
  33.9 0.1 reduce_sum.199
  34.0 0.6 fusion.21.refs_0_
  34.6 0.9 fusion.24
  35.5 0.6 copy.36
  36.1 0.6 copy.37
  36.7 9.7 %exchange_2.1 = (f32[32,1,128]{2,1,0:T(1,128)}, f32[4,512]{1,0:T(4,128)}, f32[4,512]{1,0:T(4,128)}) custom-call(f32[1,128]{1,0:T(1,128)} %fusion.21.refs_0_, f32[4,512]{1,0:T(4,128)} %bitcast.57, f32[4,512]{1,0:T(4,128)} %bitcast.56), custom_call_target="tpu_custom_call" | custom-call | tf_op jit(solution)/shard_map/exchange_2/pallas_call | solution.py:94
  46.4 0.7 broadcast_in_dim.59
  47.1 0.7 broadcast_in_dim.60
  47.8 0.9 slice_reduce_fusion.5
  48.9 0.1 reshape.246
  49.0 0.1 sub.118
  49.1 1.2 select_convert_fusion.1.act_ref
  50.4 4.3 %conv_2.1 = f32[256,512]{1,0:T(8,128)} custom-call(bf16[4,130,512]{2,1,0:T(8,128)(2,1)} %select_convert_fusion.1.act_ref, bf16[4608,512]{1,0:T(8,128)(2,1)} %bitcast.46, f32[1,512]{1,0:T(1,128)} %bitcast.58), custom_call_target="tpu_custom_call" | custom-call | flops 1207959552 | bytes 4718592 | tf_op jit(solution)/shard_map/conv_2/pallas_call | solution.py:325
  54.7 1.2 convert_reduce_fusion.1
  56.0 0.1 reduce_sum.204
  56.2 0.1 sub.123
  56.2 0.1 fusion.14
  56.4 0.1 reduce_sum.206
  56.5 0.6 fusion.22.stat_ref
  57.2 32.6 %gather_3.1 = (f32[32,1,128]{2,1,0:T(1,128)}, bf16[2,4,256,512]{3,2,1,0:T(8,128)(2,1)}, bf16[4,256,512]{2,1,0:T(8,128)(2,1)}) custom-call(f32[1,128]{1,0:T(1,128)} %fusion.22.stat_ref, bf16[256,512]{1,0:T(8,128)(2,1)} %bitcast.49), custom_call_target="tpu_custom_call" | custom-call | tf_op jit(solution)/shard_map/gather_3/pallas_call | solution.py:184
  89.8 0.9 slice_reduce_fusion.4
  91.1 2.4 %fusion.2 = bf16[2048,512]{1,0:T(8,128)(2,1)S(1)} fusion(bf16[2,4,256,512]{3,2,1,0:T(8,128)(2,1)} %get-tuple-element.34, f32[512]{0:T(512)S(1)} %copy-done.5, f32[512]{0:T(512)S(1)} %mul.115, f32[512]{0:T(512)S(1)} %sub.126), kind=kLoop, calls=%fused_computation.3 | loop fusion | flops 5242880 | bytes 4200448 | tf_op jit(solution)/shard_map/convert_element_type | solution.py:446
  93.5 1.7 %add_convert_fusion.1 = bf16[1024,512]{1,0:T(8,128)(2,1)} fusion(bf16[512,512]{1,0:T(8,128)(2,1)S(1)} %copy-done.9, bf16[1024,512]{1,0:T(8,128)(2,1)S(1)} %bitcast.61, f32[512]{0:T(512)S(1)} %copy-done.11, f32[512]{0:T(512)S(1)} %copy-done.5, f32[512]{0:T(512)S(1)} %mul.115, f32[512]{0:T(512)S(1)} %sub.126), kind=kOutput, calls=%fused_computation.11 | convolution fusion | flops 540540928 | bytes 2629632 | tf_op jit(solution)/shard_map/dot_general | solution.py:448
  95.2 2.6 %add_convert_fusion.v_ref = bf16[2048,512]{1,0:T(8,128)(2,1)} fusion(bf16[2048,512]{1,0:T(8,128)(2,1)S(1)} %fusion.2, bf16[512,512]{1,0:T(8,128)(2,1)S(1)} %copy-done, f32[512]{0:T(512)S(1)} %copy-done.12), kind=kOutput, calls=%fused_computation.4 | convolution fusion | flops 1075838976 | bytes 4720640 | tf_op jit(solution)/shard_map/dot_general | solution.py:455
  97.8 2.7 %fusion.3.k_ref = bf16[512,2048]{1,0:T(8,128)(2,1)} fusion(bf16[2048,512]{1,0:T(8,128)(2,1)S(1)} %fusion.2, bf16[512,512]{1,0:T(8,128)(2,1)S(1)} %copy-done.10), kind=kOutput, calls=%fused_computation.6 | convolution fusion | flops 1074790400 | bytes 4718592 | tf_op jit(solution)/shard_map/dot_general | solution.py:451
  100.5 23.1 %attend_4.1 = bf16[256,512]{1,0:T(8,128)(2,1)} custom-call(bf16[4,256,512]{2,1,0:T(8,128)(2,1)} %bitcast.52, bf16[512,2048]{1,0:T(8,128)(2,1)} %fusion.3.k_ref, bf16[2048,512]{1,0:T(8,128)(2,1)} %add_convert_fusion.v_ref, bf16[256,512]{1,0:T(8,128)(2,1)} %bitcast.50, bf16[512,512]{1,0:T(8,128)(2,1)} %w_ref.1, f32[1,512]{1,0:T(1,128)} %bitcast.59), custom_call_target="tpu_custom_call" | custom-call | tf_op jit(solution)/shard_map/attend_4/pallas_call | solution.py:293
  123.6 1.7 %copy.39 = bf16[2,128,512]{2,1,0:T(8,128)(2,1)} copy(bf16[2,128,512]{2,1,0:T(8,128)(2,1)} %bitcast.51) | data formatting | bytes 524288
  (65 shorter events, 1.7 us)
Async XLA Ops:
  0.0 95.2 %copy-start = (bf16[512,512]{1,0:T(8,128)(2,1)S(1)}, bf16[512,512]{1,0:T(8,128)(2,1)}, u32[]{:S(2)}) copy-start(bf16[512,512]{1,0:T(8,128)(2,1)} %param.32) | copy-start | bytes 1572868
  0.0 22.4 %copy-start.1 = (bf16[2,128,512]{2,1,0:T(8,128)(2,1)S(1)}, bf16[2,128,512]{2,1,0:T(8,128)(2,1)}, u32[]{:S(2)}) copy-start(bf16[2,128,512]{2,1,0:T(8,128)(2,1)} %refs_2_.1) | copy-start | bytes 786436
  25.2 23.8 %copy-start.6 = (f32[512]{0:T(512)S(1)}, f32[512]{0:T(512)}, u32[]{:S(2)}) copy-start(f32[512]{0:T(512)} %param.23) | copy-start | bytes 6148
  25.2 23.9 %copy-start.4 = (f32[512]{0:T(512)S(1)}, f32[512]{0:T(512)}, u32[]{:S(2)}) copy-start(f32[512]{0:T(512)} %param.24) | copy-start | bytes 6148
  31.2 18.0 %copy-start.2 = (f32[512,512]{1,0:T(8,128)S(1)}, f32[512,512]{1,0:T(8,128)}, u32[]{:S(2)}) copy-start(f32[512,512]{1,0:T(8,128)} %conv_4.1) | copy-start | bytes 3145732
  54.7 36.2 %copy-start.7 = (f32[512]{0:T(512)S(1)}, f32[512]{0:T(512)}, u32[]{:S(2)}) copy-start(f32[512]{0:T(512)} %param.27) | copy-start | bytes 6148
  54.7 36.3 %copy-start.5 = (f32[512]{0:T(512)S(1)}, f32[512]{0:T(512)}, u32[]{:S(2)}) copy-start(f32[512]{0:T(512)} %param.28) | copy-start | bytes 6148
  55.9 1.3 %copy-start.3 = (bf16[2,128,512]{2,1,0:T(8,128)(2,1)}, bf16[2,128,512]{2,1,0:T(8,128)(2,1)S(1)}, u32[]{:S(2)}) copy-start(bf16[2,128,512]{2,1,0:T(8,128)(2,1)S(1)} %get-tuple-element.42) | copy-start | bytes 786436
  91.0 2.4 %copy-start.8 = (bf16[4,256,512]{2,1,0:T(8,128)(2,1)S(1)}, bf16[4,256,512]{2,1,0:T(8,128)(2,1)}, u32[]{:S(2)}) copy-start(bf16[4,256,512]{2,1,0:T(8,128)(2,1)} %get-tuple-element.32) | copy-start | bytes 3145732
  91.1 2.4 %copy-start.9 = (bf16[512,512]{1,0:T(8,128)(2,1)S(1)}, bf16[512,512]{1,0:T(8,128)(2,1)}, u32[]{:S(2)}) copy-start(bf16[512,512]{1,0:T(8,128)(2,1)} %param.29) | copy-start | bytes 1572868
  91.1 2.4 %copy-start.11 = (f32[512]{0:T(512)S(1)}, f32[512]{0:T(512)}, u32[]{:S(2)}) copy-start(f32[512]{0:T(512)} %param.30) | copy-start | bytes 6148
  93.5 1.7 %copy-start.12 = (f32[512]{0:T(512)S(1)}, f32[512]{0:T(512)}, u32[]{:S(2)}) copy-start(f32[512]{0:T(512)} %param.33) | copy-start | bytes 6148
  95.2 2.6 %copy-start.10 = (bf16[512,512]{1,0:T(8,128)(2,1)S(1)}, bf16[512,512]{1,0:T(8,128)(2,1)}, u32[]{:S(2)}) copy-start(bf16[512,512]{1,0:T(8,128)(2,1)} %param.31) | copy-start | bytes 1572868

commit v3 on v2

--- a/solution.py
+++ b/solution.py
@@ -19,7 +19,7 @@
     return (lax.rem(tile + dt + tiles, tiles), lax.rem(head + dh + heads, heads))
 
 
-def all_barrier(tile, head, tiles, heads):
+def greet_all(tile, head, tiles, heads):
     total = tiles * heads
     me = tile * heads + head
     barrier = pltpu.get_barrier_semaphore()
@@ -32,7 +32,44 @@
         return carry
 
     lax.fori_loop(1, total, greet, 0)
-    pl.semaphore_wait(barrier, total - 1)
+
+
+def group_dot(row, onehot, axis):
+    return lax.dot_general(
+        jnp.broadcast_to(row, (8, row.shape[1])),
+        onehot,
+        (((1,), (axis,)), ((), ())),
+        precision=lax.Precision.HIGHEST,
+        preferred_element_type=jnp.float32,
+    )[:1]
+
+
+def membership():
+    channel = lax.broadcasted_iota(jnp.int32, (C, 128), 0)
+    first = lax.broadcasted_iota(jnp.int32, (C, 128), 1) * WIDTH
+    return jnp.where((channel >= first) & (channel < first + WIDTH), 1.0, 0.0)
+
+
+def store_stats(values, stat_ref):
+    onehot = membership()
+    values = values.astype(jnp.float32)
+    sums = group_dot(jnp.sum(values, axis=0, keepdims=True), onehot, 0)
+    mean = sums / (values.shape[0] * WIDTH)
+    deviation = values - group_dot(mean, onehot, 1)
+    stat_ref[0:1] = mean
+    stat_ref[1:2] = group_dot(jnp.sum(deviation * deviation, axis=0, keepdims=True), onehot, 0)
+
+
+def store_norm(slots_ref, norm_ref, count):
+    onehot = membership()
+    slots = slots_ref[...]
+    total = slots.shape[0]
+    sums = jnp.sum(slots, axis=0)
+    mean = sums[0:1] / total
+    gap = slots[:, 0:1, :] - mean[None]
+    variance = (sums[1:2] + count * jnp.sum(gap * gap, axis=0)) / (total * count)
+    norm_ref[0:1] = group_dot(mean, onehot, 1)
+    norm_ref[1:2] = group_dot(lax.rsqrt(variance + EPS), onehot, 1)
 
 
 def stats_copy(stat_ref, slots_ref, send, recv, me, total, heads, k):
@@ -48,13 +85,16 @@
 
 
 def exchange_kernel(tiles, heads, plan, npay, *refs):
-    stat_ref, pays = refs[0], refs[1 : 1 + npay]
-    slots_ref, gots = refs[1 + npay], refs[2 + npay : 2 + npay + len(plan)]
-    s_send, s_recv, p_send, p_recv = refs[2 + npay + len(plan) :]
+    values_ref, pays = refs[0], refs[1 : 1 + npay]
+    norm_ref, gots = refs[1 + npay], refs[2 + npay : 2 + npay + len(plan)]
+    stat_ref, slots_ref, s_send, s_recv, p_send, p_recv = refs[2 + npay + len(plan) :]
     total = tiles * heads
     tile, head = lax.axis_index("tile"), lax.axis_index("head")
     me = tile * heads + head
-    all_barrier(tile, head, tiles, heads)
+    greet_all(tile, head, tiles, heads)
+    store_stats(values_ref[...], stat_ref)
+    slots_ref[0] = stat_ref[...]
+    pl.semaphore_wait(pltpu.get_barrier_semaphore(), total - 1)
     copies = []
     for i, (src, dt, dh) in enumerate(plan):
         copies.append(
@@ -80,8 +120,8 @@
     lax.fori_loop(1, total, begin, 0)
     for copy in copies:
         copy.start()
-    slots_ref[0] = stat_ref[...]
     lax.fori_loop(1, total, finish, 0)
+    store_norm(slots_ref, norm_ref, values_ref.shape[0] * WIDTH)
     for copy in copies:
         copy.wait()
 
@@ -89,7 +129,7 @@
 def exchange(cid, stat, payloads, plan):
     tiles, heads = lax.axis_size("tile"), lax.axis_size("head")
     total = tiles * heads
-    outs = [jax.ShapeDtypeStruct((total, 1, 128), jnp.float32)]
+    outs = [jax.ShapeDtypeStruct((2, C), jnp.float32)]
     outs += [jax.ShapeDtypeStruct(payloads[s].shape, payloads[s].dtype) for s, _, _ in plan]
     return pl.pallas_call(
         functools.partial(exchange_kernel, tiles, heads, plan, len(payloads)),
@@ -97,6 +137,8 @@
         in_specs=[VMEM] * (1 + len(payloads)),
         out_specs=[VMEM] * len(outs),
         scratch_shapes=[
+            pltpu.VMEM((2, 128), jnp.float32),
+            pltpu.VMEM((total, 2, 128), jnp.float32),
             pltpu.SemaphoreType.DMA((total,)),
             pltpu.SemaphoreType.DMA((total,)),
             pltpu.SemaphoreType.DMA((len(plan),)),
@@ -107,13 +149,18 @@
     )(stat, *payloads)
 
 
-def gather_kernel(tiles, heads, stat_ref, res_ref, slots_ref, kv_ref, q_ref, *sems):
+def gather_kernel(
+    tiles, heads, res_ref, norm_ref, kv_ref, q_ref, stat_ref, slots_ref, *sems
+):
     s_send, s_recv, z_send, z_recv, c_send, c_recv, q_send, q_recv = sems
     total = tiles * heads
     tile, head = lax.axis_index("tile"), lax.axis_index("head")
     me = tile * heads + head
     partner = (tile + 1 - 2 * lax.rem(tile, 2), head)
-    all_barrier(tile, head, tiles, heads)
+    greet_all(tile, head, tiles, heads)
+    store_stats(res_ref[...], stat_ref)
+    slots_ref[0] = stat_ref[...]
+    pl.semaphore_wait(pltpu.get_barrier_semaphore(), total - 1)
     one = functools.partial(stats_copy, stat_ref, slots_ref, s_send, s_recv, me, total, heads)
 
     def begin(k, carry):
@@ -163,8 +210,8 @@
     ccopy(0).start()
     kv_ref[0, 0] = res_ref[...]
     q_ref[0] = res_ref[...]
-    slots_ref[0] = stat_ref[...]
     lax.fori_loop(1, total, finish, 0)
+    store_norm(slots_ref, norm_ref, res_ref.shape[0] * WIDTH)
     for k in range(1, heads):
         zcopy(k).wait_recv()
         ccopy(k).start()
@@ -176,7 +223,7 @@
         ccopy(k).wait()
 
 
-def gather(cid, stat, resid):
+def gather(cid, resid):
     tiles, heads = lax.axis_size("tile"), lax.axis_size("head")
     total = tiles * heads
     n, c = resid.shape
@@ -184,19 +231,23 @@
     return pl.pallas_call(
         functools.partial(gather_kernel, tiles, heads),
         out_shape=[
-            jax.ShapeDtypeStruct((total, 1, 128), jnp.float32),
+            jax.ShapeDtypeStruct((2, C), jnp.float32),
             jax.ShapeDtypeStruct((2, heads, n, c), resid.dtype),
             jax.ShapeDtypeStruct((tiles // 2, n, c), resid.dtype),
         ],
-        in_specs=[VMEM] * 2,
+        in_specs=[VMEM],
         out_specs=[VMEM] * 3,
-        scratch_shapes=[dma((total,))] * 2
+        scratch_shapes=[
+            pltpu.VMEM((2, 128), jnp.float32),
+            pltpu.VMEM((total, 2, 128), jnp.float32),
+        ]
+        + [dma((total,))] * 2
         + [dma((heads,))] * 4
         + [dma((tiles // 2,))] * 2,
 
         compiler_params=pltpu.CompilerParams(collective_id=cid, has_side_effects=True),
         name="gather_%d" % cid,
-    )(stat, resid)
+    )(resid)
 
 
 def attend_kernel(
@@ -341,26 +392,8 @@
     return out.reshape(rows, cols, C)
 
 
-def spread(per_group):
-    return jnp.broadcast_to(per_group[:, None], (GROUPS, WIDTH)).reshape(C)
-
-
-def local_stats(flat):
-    count = flat.shape[0] * WIDTH
-    mean = jnp.sum(jnp.sum(flat, axis=0).reshape(GROUPS, WIDTH), axis=1) / count
-    deviation = flat - spread(mean)
-    square = jnp.sum(jnp.sum(deviation * deviation, axis=0).reshape(GROUPS, WIDTH), axis=1)
-    pad = jnp.zeros((128 - 2 * GROUPS,), jnp.float32)
-    return jnp.concatenate([mean, square, pad]).reshape(1, 128)
-
-
-def combined(slots, count, gain, shift):
-    total = slots.shape[0]
-    means, squares = slots[:, 0, :GROUPS], slots[:, 0, GROUPS : 2 * GROUPS]
-    mean = jnp.sum(means, axis=0) / total
-    gap = means - mean[None]
-    variance = (jnp.sum(squares, axis=0) + count * jnp.sum(gap * gap, axis=0)) / (total * count)
-    return spread(mean), spread(lax.rsqrt(variance + EPS)) * gain, shift
+def combined(norm, gain, shift):
+    return norm[0], norm[1] * gain, shift
 
 
 def normalize(values, norm):
@@ -398,7 +431,6 @@
     tiles, heads = lax.axis_size("tile"), lax.axis_size("head")
     tile, head = lax.axis_index("tile"), lax.axis_index("head")
     n = rows * cols
-    count = n * WIDTH
     latent32 = latent.astype(jnp.float32)
 
     top, bottom = latent[:2], latent[rows - 2 :]
@@ -415,7 +447,7 @@
         (4, -1, -1),
     )
     slots, above, below, left, right, al, ar, bl, br = exchange(
-        1, local_stats(latent32.reshape(n, C)), payloads, plan
+        1, latent.reshape(n, C), payloads, plan
     )
     lefts = jnp.concatenate([al, left, bl], axis=0)[:, None]
     rights = jnp.concatenate([ar, right, br], axis=0)[:, None]
@@ -423,26 +455,26 @@
     wide = jnp.concatenate([lefts, middle, rights], axis=1).astype(jnp.float32)
     first_row, first_col = tile * rows, head * cols
     all_rows, all_cols = rows * tiles, cols * heads
-    act1 = jax.nn.silu(normalize(wide, combined(slots, count, norm1_gain, norm1_shift)))
+    act1 = jax.nn.silu(normalize(wide, combined(slots, norm1_gain, norm1_shift)))
     mask1 = inside(rows + 4, cols + 2, first_row - 2, first_col - 1, all_rows, all_cols)
     act1 = jnp.where(mask1, act1, 0.0).astype(jnp.bfloat16)
     hidden = conv(act1, conv1_weight, conv1_bias)
 
     slots, left, right = exchange(
         2,
-        local_stats(hidden[1 : rows + 1].reshape(n, C)),
+        hidden[1 : rows + 1].reshape(n, C),
         [hidden[:, 0], hidden[:, cols - 1]],
         ((1, 0, 1), (0, 0, -1)),
     )
     wide = jnp.concatenate([left[:, None], hidden, right[:, None]], axis=1)
-    act2 = jax.nn.silu(normalize(wide, combined(slots, count, norm2_gain, norm2_shift)))
+    act2 = jax.nn.silu(normalize(wide, combined(slots, norm2_gain, norm2_shift)))
     mask2 = inside(rows + 2, cols + 2, first_row - 1, first_col - 1, all_rows, all_cols)
     act2 = jnp.where(mask2, act2, 0.0).astype(jnp.bfloat16)
     resid = (latent32 + conv(act2, conv2_weight, conv2_bias)).astype(jnp.bfloat16)
     resid = resid.reshape(n, C)
 
-    slots, kv_res, q_res = gather(3, local_stats(resid.astype(jnp.float32)), resid)
-    norm3 = combined(slots, count, norm3_gain, norm3_shift)
+    slots, kv_res, q_res = gather(3, resid)
+    norm3 = combined(slots, norm3_gain, norm3_shift)
     kv_in = normalize(kv_res.reshape(-1, C).astype(jnp.float32), norm3).astype(jnp.bfloat16)
     q_in = normalize(q_res.reshape(-1, C).astype(jnp.float32), norm3).astype(jnp.bfloat16)
     queries = (jnp.dot(q_in, query_weight, preferred_element_type=jnp.float32) + query_bias).astype(

time: 126 us -> 121 us (0.960)
  other arithmetic: 19.7 us -> 10.5 us
  local copies, waits for them, and re-layouts: 8.43 us -> 10.8 us
  Pallas kernels: 90 us -> 91.5 us
    reduce_sum x18 -> x0, other arithmetic: 9.17 us -> none  [the longest x6 3.71 us: local_stats(): mean = jnp.sum(jnp.sum(flat, axis=0).reshape(GROUPS, WIDTH), axis=1) / count]
    slice x0 -> x4, local copies, waits for them, and re-layouts: none -> 4.16 us  [the longest x3 2.28 us: combined(): return (norm[0], norm[1] * gain, shift)]
    convert_element_type x0 -> x1, other arithmetic: none -> 1.81 us  [per_device(): (latent32 + conv(act2, conv2_weight, conv2_bias)).astype(jnp.bfloat16)]
    reshape x3 -> x0, other arithmetic: 1.78 us -> none  [local_stats(): return jnp.concatenate([mean, square, pad]).reshape(1, 128)]
    pallas_call x2, Pallas kernels: 24 us -> 25.3 us  [exchange(): pl.pallas_call(functools.partial(exchange_kernel, tiles, heads, plan, len...]
    unnamed x29 -> x27, local copies, waits for them, and re-layouts: 2.93 us -> 2.92 us
where the time goes in v3:
time: 121 us; the launch traced here: 120 us
  Pallas kernels  91.5 us (76%)
  local copies, waits for them, and re-layouts  10.8 us (9%)
  other arithmetic  10.5 us (9%)
  matrix products  6.95 us (6%)
    pallas_call x1, Pallas kernels, gather(): pl.pallas_call(functools.partial(gather_kernel, tiles, heads), out_shape=...  32.7 us
    pallas_call x2, Pallas kernels, exchange(): pl.pallas_call(functools.partial(exchange_kernel, tiles, heads, plan, len...  25.3 us
    pallas_call x1, Pallas kernels, attend(): pl.pallas_call(functools.partial(attend_kernel, tiles, heads), out_shape=...  23.2 us
    pallas_call x2, Pallas kernels, conv(): pl.pallas_call(conv_kernel, grid=(C // part,), out_shape=jax.ShapeDtypeSt...  10.3 us
    unnamed x27, local copies, waits for them, and re-layouts  2.92 us
    convert_element_type x1, other arithmetic, per_device(): act1 = jnp.where(mask1, act1, 0.0).astype(jnp.bfloat16)  2.83 us
    dot_general x1, matrix products, per_device(): lax.dot_general(key_weight, kv_in, (((0,), (1,)), ((), ())), preferred_el...  2.66 us
    dot_general x1, matrix products, per_device(): jnp.dot(kv_in, value_weight, preferred_element_type=jnp.float32)  2.59 us

profile of v3, /device:TPU:8, one launch (start us, length us, event | category | flops | bytes accessed | tf_op | source)
XLA Modules:
  0.0 120.0 jit_solution(18160799596518748196)
XLA Ops:
  0.0 0.0 copy-start
  0.0 0.1 and_and_fusion.1
  0.1 0.1 and_and_fusion
  0.2 0.7 fusion.16
  0.9 0.6 copy_bitcast_fusion.2
  1.5 14.6 %exchange_1.1 = (f32[2,512]{1,0:T(2,128)}, bf16[2,128,512]{2,1,0:T(8,128)(2,1)}, bf16[2,128,512]{2,1,0:T(8,128)(2,1)}, bf16[2,512]{1,0:T(2,128)(2,1)}, bf16[2,51...) custom-call(bf16[256,512]{1,0:T(8,128)(2,1)} %bitcast.43, ...), custom_call_target="tpu_custom_call" | custom-call | tf_op jit(solution)/shard_map/exchange_1/pallas_call | solution.py:134
  16.2 0.7 maximum_bitcast_fusion
  16.9 0.8 fusion.19
  17.6 0.7 mul.57
  18.3 0.7 maximum_bitcast_fusion.1
  19.0 2.8 %select_convert_fusion.act_ref = bf16[6,130,512]{2,1,0:T(8,128)(2,1)} fusion(bf16[6,1,512]{2,1,0:T(2,128)(2,1)S(1)} %copy.25, bf16[2,128,512]{2,1,0:T(8,128)(2,1)} %get-tuple-element.24, bf16[2,128,512]{2,1,0:T(8,128)(2,1)} %refs_2_.1, bf16[2,128,512]{2,1,0:T(8,128)(2,1)} %get-tuple-element.23, bf16[6,1,512]{2,1,0:T(2,128)(2,1)S(1)} %copy.24, f32[512]{0:T(512)} %param.20, ...), kind=kLoop, calls=%fused_computation.12 | loop fusion | flops 7587840 | bytes 1604364 | tf_op jit(solution)/shard_map/convert_element_type | solution.py:460
  21.9 5.9 %conv_4.1 = f32[512,512]{1,0:T(8,128)} custom-call(bf16[6,130,512]{2,1,0:T(8,128)(2,1)} %select_convert_fusion.act_ref, bf16[4608,512]{1,0:T(8,128)(2,1)} %bitcast.63, f32[1,512]{1,0:T(1,128)} %bitcast.65), custom_call_target="tpu_custom_call" | custom-call | flops 2415919104 | bytes 4718592 | tf_op jit(solution)/shard_map/conv_4/pallas_call | solution.py:376
  27.8 0.0 copy-start.5
  27.8 1.0 fusion.15
  28.8 0.6 copy.36
  29.4 0.6 copy.37
  30.0 1.9 %slice.45.refs_0_ = f32[256,512]{1,0:T(8,128)} slice(f32[512,512]{1,0:T(8,128)} %conv_4.1), slice={[128:384], [0:512]} | slice | bytes 1048576 | tf_op jit(solution)/shard_map/slice | solution.py:465
  31.9 10.7 %exchange_2.1 = (f32[2,512]{1,0:T(2,128)}, f32[4,512]{1,0:T(4,128)}, f32[4,512]{1,0:T(4,128)}) custom-call(f32[256,512]{1,0:T(8,128)} %slice.45.refs_0_, f32[4,512]{1,0:T(4,128)} %bitcast.53, f32[4,512]{1,0:T(4,128)} %bitcast.52), custom_call_target="tpu_custom_call" | custom-call | tf_op jit(solution)/shard_map/exchange_2/pallas_call | solution.py:134
  42.6 0.7 broadcast_in_dim.51
  43.3 0.8 fusion.18
  44.0 0.0 copy-done.5
  44.0 0.7 broadcast_in_dim.52
  44.7 0.0 copy-done.2
  44.7 0.0 copy-done.3
  44.8 1.3 %select_convert_fusion.1.act_ref = bf16[4,130,512]{2,1,0:T(8,128)(2,1)} fusion(f32[4,1,512]{2,1,0:T(1,128)S(1)} %broadcast_in_dim.52, f32[4,128,512]{2,1,0:T(8,128)S(1)} %bitcast.46, f32[4,1,512]{2,1,0:T(1,128)S(1)} %broadcast_in_dim.51, f32[512]{0:T(512)S(1)} %copy-done.3, f32[512]{0:T(512)S(1)} %mul.61, f32[512]{0:T(512)S(1)} %bitcast.55, ...), kind=kLoop, calls=%fused_computation.16 | loop fusion | flops 2928640 | bytes 1604104 | tf_op jit(solution)/shard_map/convert_element_type | solution.py:472
  46.0 4.4 %conv_2.1 = f32[256,512]{1,0:T(8,128)} custom-call(bf16[4,130,512]{2,1,0:T(8,128)(2,1)} %select_convert_fusion.1.act_ref, bf16[4608,512]{1,0:T(8,128)(2,1)} %bitcast.44, f32[1,512]{1,0:T(1,128)} %bitcast.61), custom_call_target="tpu_custom_call" | custom-call | flops 1207959552 | bytes 4718592 | tf_op jit(solution)/shard_map/conv_2/pallas_call | solution.py:376
  50.4 0.0 copy-done.1
  50.4 1.8 %add_convert_fusion.2 = bf16[2,128,512]{2,1,0:T(8,128)(2,1)} fusion(f32[2,128,512]{2,1,0:T(8,128)} %bitcast.49, bf16[2,128,512]{2,1,0:T(8,128)(2,1)S(1)} %copy-done.1), kind=kLoop, calls=%fused_computation.20 | loop fusion | flops 393216 | bytes 1048576 | tf_op jit(solution)/shard_map/convert_element_type | solution.py:473
  52.2 32.7 %gather_3.1 = (f32[2,512]{1,0:T(2,128)}, bf16[2,4,256,512]{3,2,1,0:T(8,128)(2,1)}, bf16[4,256,512]{2,1,0:T(8,128)(2,1)}) custom-call(bf16[256,512]{1,0:T(8,128)(2,1)} %bitcast.47), custom_call_target="tpu_custom_call" | custom-call | tf_op jit(solution)/shard_map/gather_3/pallas_call | solution.py:231
  84.9 0.8 fusion.17
  85.7 0.0 copy-done.6
  85.7 0.0 copy-done.4
  85.7 0.0 copy-start.7
  85.7 0.0 copy-start.8
  85.8 0.0 copy-start.10
  85.8 2.4 %fusion.2 = bf16[2048,512]{1,0:T(8,128)(2,1)S(1)} fusion(bf16[2,4,256,512]{3,2,1,0:T(8,128)(2,1)} %get-tuple-element.34, f32[512]{0:T(512)S(1)} %copy-done.4, f32[512]{0:T(512)S(1)} %mul.65, f32[512]{0:T(512)S(1)} %bitcast.56), kind=kLoop, calls=%fused_computation.3 | loop fusion | flops 5242880 | bytes 4200448 | tf_op jit(solution)/shard_map/convert_element_type | solution.py:478
  88.1 0.0 copy-done.7
  88.1 0.0 copy-done.8
  88.2 0.0 copy-done.10
  88.2 0.0 copy-start.11
  88.2 1.7 %add_convert_fusion.1 = bf16[1024,512]{1,0:T(8,128)(2,1)} fusion(bf16[512,512]{1,0:T(8,128)(2,1)S(1)} %copy-done.8, bf16[1024,512]{1,0:T(8,128)(2,1)S(1)} %bitcast.64, f32[512]{0:T(512)S(1)} %copy-done.10, f32[512]{0:T(512)S(1)} %copy-done.4, f32[512]{0:T(512)S(1)} %mul.65, f32[512]{0:T(512)S(1)} %bitcast.57), kind=kOutput, calls=%fused_computation.11 | convolution fusion | flops 540540928 | bytes 2629632 | tf_op jit(solution)/shard_map/dot_general | solution.py:480
  89.9 0.0 copy-done
  89.9 0.0 copy-done.11
  89.9 2.6 %add_convert_fusion.v_ref = bf16[2048,512]{1,0:T(8,128)(2,1)} fusion(bf16[2048,512]{1,0:T(8,128)(2,1)S(1)} %fusion.2, bf16[512,512]{1,0:T(8,128)(2,1)S(1)} %copy-done, f32[512]{0:T(512)S(1)} %copy-done.11), kind=kOutput, calls=%fused_computation.4 | convolution fusion | flops 1075838976 | bytes 4720640 | tf_op jit(solution)/shard_map/dot_general | solution.py:487
  92.5 0.0 copy-done.9
  92.5 2.7 %fusion.3.k_ref = bf16[512,2048]{1,0:T(8,128)(2,1)} fusion(bf16[2048,512]{1,0:T(8,128)(2,1)S(1)} %fusion.2, bf16[512,512]{1,0:T(8,128)(2,1)S(1)} %copy-done.9), kind=kOutput, calls=%fused_computation.6 | convolution fusion | flops 1074790400 | bytes 4718592 | tf_op jit(solution)/shard_map/dot_general | solution.py:483
  95.1 23.2 %attend_4.1 = bf16[256,512]{1,0:T(8,128)(2,1)} custom-call(bf16[4,256,512]{2,1,0:T(8,128)(2,1)} %bitcast.51, bf16[512,2048]{1,0:T(8,128)(2,1)} %fusion.3.k_ref, bf16[2048,512]{1,0:T(8,128)(2,1)} %add_convert_fusion.v_ref, bf16[256,512]{1,0:T(8,128)(2,1)} %bitcast.48, bf16[512,512]{1,0:T(8,128)(2,1)} %w_ref.1, f32[1,512]{1,0:T(1,128)} %bitcast.62), custom_call_target="tpu_custom_call" | custom-call | tf_op jit(solution)/shard_map/attend_4/pallas_call | solution.py:344
  118.3 1.7 %copy.39 = bf16[2,128,512]{2,1,0:T(8,128)(2,1)} copy(bf16[2,128,512]{2,1,0:T(8,128)(2,1)} %bitcast.50) | data formatting | bytes 524288
  (13 shorter events, 0.1 us)
Async XLA Ops:
  0.0 89.9 %copy-start = (bf16[512,512]{1,0:T(8,128)(2,1)S(1)}, bf16[512,512]{1,0:T(8,128)(2,1)}, u32[]{:S(2)}) copy-start(bf16[512,512]{1,0:T(8,128)(2,1)} %param.32) | copy-start | bytes 1572868
  27.8 16.2 %copy-start.5 = (f32[512]{0:T(512)S(1)}, f32[512]{0:T(512)}, u32[]{:S(2)}) copy-start(f32[512]{0:T(512)} %param.23) | copy-start | bytes 6148
  27.8 16.9 %copy-start.2 = (f32[512,512]{1,0:T(8,128)S(1)}, f32[512,512]{1,0:T(8,128)}, u32[]{:S(2)}) copy-start(f32[512,512]{1,0:T(8,128)} %conv_4.1) | copy-start | bytes 3145732
  27.8 16.9 %copy-start.3 = (f32[512]{0:T(512)S(1)}, f32[512]{0:T(512)}, u32[]{:S(2)}) copy-start(f32[512]{0:T(512)} %param.24) | copy-start | bytes 6148
  46.0 4.4 %copy-start.1 = (bf16[2,128,512]{2,1,0:T(8,128)(2,1)S(1)}, bf16[2,128,512]{2,1,0:T(8,128)(2,1)}, u32[]{:S(2)}) copy-start(bf16[2,128,512]{2,1,0:T(8,128)(2,1)} %refs_2_.1) | copy-start | bytes 786436
  46.0 39.7 %copy-start.6 = (f32[512]{0:T(512)S(1)}, f32[512]{0:T(512)}, u32[]{:S(2)}) copy-start(f32[512]{0:T(512)} %param.27) | copy-start | bytes 6148
  46.0 39.7 %copy-start.4 = (f32[512]{0:T(512)S(1)}, f32[512]{0:T(512)}, u32[]{:S(2)}) copy-start(f32[512]{0:T(512)} %param.28) | copy-start | bytes 6148
  85.7 2.4 %copy-start.7 = (bf16[4,256,512]{2,1,0:T(8,128)(2,1)S(1)}, bf16[4,256,512]{2,1,0:T(8,128)(2,1)}, u32[]{:S(2)}) copy-start(bf16[4,256,512]{2,1,0:T(8,128)(2,1)} %get-tuple-element.32) | copy-start | bytes 3145732
  85.7 2.4 %copy-start.8 = (bf16[512,512]{1,0:T(8,128)(2,1)S(1)}, bf16[512,512]{1,0:T(8,128)(2,1)}, u32[]{:S(2)}) copy-start(bf16[512,512]{1,0:T(8,128)(2,1)} %param.29) | copy-start | bytes 1572868
  85.8 2.4 %copy-start.10 = (f32[512]{0:T(512)S(1)}, f32[512]{0:T(512)}, u32[]{:S(2)}) copy-start(f32[512]{0:T(512)} %param.30) | copy-start | bytes 6148
  88.2 1.7 %copy-start.11 = (f32[512]{0:T(512)S(1)}, f32[512]{0:T(512)}, u32[]{:S(2)}) copy-start(f32[512]{0:T(512)} %param.33) | copy-start | bytes 6148
  89.9 2.6 %copy-start.9 = (bf16[512,512]{1,0:T(8,128)(2,1)S(1)}, bf16[512,512]{1,0:T(8,128)(2,1)}, u32[]{:S(2)}) copy-start(bf16[512,512]{1,0:T(8,128)(2,1)} %param.31) | copy-start | bytes 1572868
